TPU v7x, 256 devices: a whole 4x4x8 slice. The times are simulated.
256 devices in a mesh: bank: 32 (over z_hi, y, x), lane: 8 (over z_lo, core).
Axes of the slice: x: 4, y: 4, z: 8 (z_hi: 2, z_lo: 4; z = z_hi * 4 + z_lo), core: 2. Of those that a mesh axis runs over, the one named last changes fastest.
Arguments:
- amplitudes: float32 [2, 1024, 128, 128], P(None, ('bank', 'lane')), may hold values from -6 to 6
- energies: float32 [1024, 128, 128], P(('bank', 'lane')), may hold values from -2 to 2
- phase_angles: float32 [2, 128], replicated, may hold values from 0.3 to 1.2
- mix_angles: float32 [2, 4], replicated, may hold values from 0.3 to 1.2
Outputs:
- final_parts: float32 [2, 1024, 128, 128], P(None, ('bank', 'lane'))
- marginal: float32 [32, 128, 128], P('lane', 'bank')
All inputs are finite; a program needn't handle non-finite values.
Results may differ from a plain program's by a relative error of at most 0.0003.
Values sent between devices are 32-bit elements; how exact they have to be, the bound alone decides.
No kernel may reach another device: no remote copies, remote signals or barrier semaphores. Data moves between devices by JAX's collectives and lax.ppermute only.
A program may use at most 64 MiB of HBM per device.

v0:
```python
import jax
import jax.numpy as jnp
from jax import lax
from jax.sharding import PartitionSpec as P

LAYERS = 2


def cut_along(value, dim, length):
    shape = value.shape
    parts = value.reshape(*shape[:dim], length, shape[dim] // length, *shape[dim + 1 :])
    return jnp.moveaxis(parts, dim, 0)


def sent_and_summed(value, axis, dim):
    length = lax.axis_size(axis)
    parts = lax.all_to_all(cut_along(value, dim, length), axis, 0, 0, tiled=True)
    return jnp.sum(parts, axis=0)


def count_bits(values, count):
    places = jnp.arange(count.bit_length() - 1, dtype=jnp.int32)
    return jnp.sum(values[..., None] >> places & 1, axis=-1)


def turn_table(count, angle):
    rank = jnp.arange(count, dtype=jnp.int32)
    apart = count_bits(rank[:, None] ^ rank[None, :], count)
    bits = count.bit_length() - 1
    size = jnp.cos(angle) ** (bits - apart).astype(jnp.float32) * jnp.sin(angle) ** apart.astype(
        jnp.float32
    )
    real_sign = jnp.where(apart % 4 == 0, 1.0, jnp.where(apart % 4 == 2, -1.0, 0.0)).astype(
        jnp.float32
    )
    imag_sign = jnp.where(apart % 4 == 1, -1.0, jnp.where(apart % 4 == 3, 1.0, 0.0)).astype(
        jnp.float32
    )
    return (size * real_sign, size * imag_sign)


def apply_along(values, dim, angle):
    real_part, imag_part = turn_table(values.shape[dim], angle)

    def times(table):
        moved = jnp.tensordot(values, table, axes=([dim], [0]), precision=lax.Precision.HIGHEST)
        return jnp.moveaxis(moved, -1, dim)

    by_real = times(real_part)
    by_imag = times(imag_part)
    return jnp.stack([by_real[0] - by_imag[1], by_real[1] + by_imag[0]])


def diagonal_step(values, levels, angle):
    turn = angle * levels
    return jnp.stack(
        [
            values[0] * jnp.cos(turn) + values[1] * jnp.sin(turn),
            values[1] * jnp.cos(turn) - values[0] * jnp.sin(turn),
        ]
    )


def on_device(amplitudes, energies, phase_angles, mix_angles):
    values = amplitudes
    for layer in range(LAYERS):
        values = diagonal_step(values, energies, phase_angles[layer])
        values = apply_along(values, 3, mix_angles[layer, 0])
        values = apply_along(values, 2, mix_angles[layer, 1])
        moved = lax.all_to_all(values, "bank", split_axis=2, concat_axis=1, tiled=True)
        moved = apply_along(moved, 1, mix_angles[layer, 2])
        values = lax.all_to_all(moved, "bank", split_axis=1, concat_axis=2, tiled=True)
        moved = lax.all_to_all(values, "lane", split_axis=3, concat_axis=1, tiled=True)
        spread = moved.reshape(2, lax.axis_size("lane"), -1, moved.shape[2], moved.shape[3])
        moved = apply_along(spread, 1, mix_angles[layer, 3]).reshape(moved.shape)
        values = lax.all_to_all(moved, "lane", split_axis=1, concat_axis=3, tiled=True)
    chance = values[0] * values[0] + values[1] * values[1]
    marginal = sent_and_summed(chance, "bank", 1) / lax.axis_size("bank")
    return (values, marginal)


def solution(mesh):
    placed = (P(None, ("bank", "lane"), None, None), P(("bank", "lane"), None, None), P(), P())
    return jax.shard_map(
        on_device,
        mesh=mesh,
        in_specs=placed,
        out_specs=(P(None, ("bank", "lane"), None, None), P("lane", "bank", None)),
        check_vma=False,
    )
```

profile of v0, /device:TPU:1, one launch (start us, length us, event | category | flops | bytes accessed | tf_op | source)
XLA Modules:
  0.0 226.1 jit_solution(11334041736106467783)
XLA Ops:
  0.6 1.7 fusion.220
  6.0 2.1 fusion.14
  9.7 1.1 convolution_bitcast_fusion.10
  10.8 1.1 convolution_bitcast_fusion.11
  12.0 1.0 copy.91
  13.0 14.5 %all-to-all-start = ((f32[2,4,128,128]{3,1,0,2:T(4,128)}), f32[2,4,128,128]{3,1,0,2:T(4,128)S(1)}, u32[]{:S(2)}, u32[]{:S(2)}) async-start(f32[2,4,128,128]{3,1,0,2:T(4,128)} %copy.91), calls=%async_computation | async-start | bytes 1048576 | tf_op jit(solution)/shard_map/all_to_all | solution.py:70
  28.9 12.5 %all-to-all-done = f32[2,4,128,128]{3,1,0,2:T(4,128)S(1)} async-done(((f32[2,4,128,128]{3,1,0,2:T(4,128)}), f32[2,4,128,128]{3,1,0,2:T(4,128)S(1)}, u32[]{:S(2)}, u32[]{:S(2)}) %all-to-all-start) | async-done | bytes 524320 | tf_op jit(solution)/shard_map/all_to_all | solution.py:70
  41.8 1.1 convolution_bitcast_fusion.8
  42.9 1.1 convolution_bitcast_fusion.9
  44.4 17.6 %all_to_all.140 = f32[2,128,4,128]{3,2,0,1:T(4,128)S(1)} all-to-all(f32[2,128,4,128]{3,2,0,1:T(4,128)S(1)} %copy.96), channel_id=1, replica_groups=mesh['bank'=32,'lane'=8] {'bank'}, dimensions={1} | all-to-all | bytes 1048576 | tf_op jit(solution)/shard_map/all_to_all | solution.py:72
  62.4 1.0 copy.99
  63.4 13.3 %all-to-all-start.2 = ((f32[2,4,128,128]{2,1,0,3:T(4,128)}), f32[2,4,128,128]{2,1,0,3:T(4,128)S(1)}, u32[]{:S(2)}, u32[]{:S(2)}) async-start(f32[2,4,128,128]{2,1,0,3:T(4,128)} %copy.99), calls=%async_computation.2 | async-start | bytes 1048576 | tf_op jit(solution)/shard_map/all_to_all | solution.py:73
  78.0 13.1 %all-to-all-done.2 = f32[2,4,128,128]{2,1,0,3:T(4,128)S(1)} async-done(((f32[2,4,128,128]{2,1,0,3:T(4,128)}), f32[2,4,128,128]{2,1,0,3:T(4,128)S(1)}, u32[]{:S(2)}, u32[]{:S(2)}) %all-to-all-start.2) | async-done | bytes 524320 | tf_op jit(solution)/shard_map/all_to_all | solution.py:73
  92.0 0.9 convolution_bitcast_fusion.7
  94.0 4.4 %all-to-all-start.3 = ((f32[2,32,128,16]{2,3,0,1:T(8,128)}), f32[2,32,128,16]{2,3,0,1:T(8,128)S(1)}, u32[]{:S(2)}, u32[]{:S(2)}) async-start(f32[2,32,128,16]{2,3,0,1:T(8,128)} %copy.106), calls=%async_computation.3 | async-start | bytes 1048576 | tf_op jit(solution)/shard_map/all_to_all | solution.py:76
  101.4 11.3 %all-to-all-done.3 = f32[2,32,128,16]{2,3,0,1:T(8,128)S(1)} async-done(((f32[2,32,128,16]{2,3,0,1:T(8,128)}), f32[2,32,128,16]{2,3,0,1:T(8,128)S(1)}, u32[]{:S(2)}, u32[]{:S(2)}) %all-to-all-start.3) | async-done | bytes 524320 | tf_op jit(solution)/shard_map/all_to_all | solution.py:76
  113.2 1.0 add_bitcast_fusion
  115.8 1.1 convolution_bitcast_fusion.4
  116.9 1.1 convolution_bitcast_fusion.5
  118.1 1.0 copy.116
  119.1 3.9 %all-to-all-start.4 = ((f32[2,4,128,128]{3,1,0,2:T(4,128)}), f32[2,4,128,128]{3,1,0,2:T(4,128)S(1)}, u32[]{:S(2)}, u32[]{:S(2)}) async-start(f32[2,4,128,128]{3,1,0,2:T(4,128)} %copy.116), calls=%async_computation.4 | async-start | bytes 1048576 | tf_op jit(solution)/shard_map/all_to_all | solution.py:70
  124.3 15.1 %all-to-all-done.4 = f32[2,4,128,128]{3,1,0,2:T(4,128)S(1)} async-done(((f32[2,4,128,128]{3,1,0,2:T(4,128)}), f32[2,4,128,128]{3,1,0,2:T(4,128)S(1)}, u32[]{:S(2)}, u32[]{:S(2)}) %all-to-all-start.4) | async-done | bytes 524320 | tf_op jit(solution)/shard_map/all_to_all | solution.py:70
  139.8 1.1 convolution_bitcast_fusion.2
  140.9 1.1 convolution_bitcast_fusion.3
  142.4 19.9 %all_to_all.141 = f32[2,128,4,128]{3,2,0,1:T(4,128)S(1)} all-to-all(f32[2,128,4,128]{3,2,0,1:T(4,128)S(1)} %copy.121), channel_id=1, replica_groups=mesh['bank'=32,'lane'=8] {'bank'}, dimensions={1} | all-to-all | bytes 1048576 | tf_op jit(solution)/shard_map/all_to_all | solution.py:72
  162.8 1.0 copy.124
  163.8 7.0 %all-to-all-start.6 = ((f32[2,4,128,128]{2,1,0,3:T(4,128)}), f32[2,4,128,128]{2,1,0,3:T(4,128)S(1)}, u32[]{:S(2)}, u32[]{:S(2)}) async-start(f32[2,4,128,128]{2,1,0,3:T(4,128)} %copy.124), calls=%async_computation.6 | async-start | bytes 1048576 | tf_op jit(solution)/shard_map/all_to_all | solution.py:73
  172.2 12.9 %all-to-all-done.6 = f32[2,4,128,128]{2,1,0,3:T(4,128)S(1)} async-done(((f32[2,4,128,128]{2,1,0,3:T(4,128)}), f32[2,4,128,128]{2,1,0,3:T(4,128)S(1)}, u32[]{:S(2)}, u32[]{:S(2)}) %all-to-all-start.6) | async-done | bytes 524320 | tf_op jit(solution)/shard_map/all_to_all | solution.py:73
  187.3 17.7 %all_to_all.142 = f32[2,32,128,16]{2,3,0,1:T(8,128)S(1)} all-to-all(f32[2,32,128,16]{2,3,0,1:T(8,128)S(1)} %copy.131), channel_id=1, replica_groups=mesh['bank'=32,'lane'=8] {'lane'}, dimensions={1} | all-to-all | bytes 1048576 | tf_op jit(solution)/shard_map/all_to_all | solution.py:76
  207.1 6.4 %all-to-all-start.8 = ((f32[32,4,4,128]{3,2,1,0:T(4,128)}), f32[32,4,4,128]{3,2,1,0:T(4,128)S(1)}, u32[]{:S(2)}, u32[]{:S(2)}) async-start(f32[32,4,4,128]{3,2,1,0:T(4,128)} %copy.135), calls=%async_computation.8 | async-start | bytes 524288 | tf_op jit(solution)/shard_map/all_to_all | solution.py:17
  213.6 1.0 copy.136
  214.6 10.9 %all-to-all-done.8 = f32[32,4,4,128]{3,2,1,0:T(4,128)S(1)} async-done(((f32[32,4,4,128]{3,2,1,0:T(4,128)}), f32[32,4,4,128]{3,2,1,0:T(4,128)S(1)}, u32[]{:S(2)}, u32[]{:S(2)}) %all-to-all-start.8) | async-done | bytes 262176 | tf_op jit(solution)/shard_map/all_to_all | solution.py:17
  (58 shorter events, 13.9 us)
Async XLA Ops:
  13.0 28.4 %all-to-all-start = ((f32[2,4,128,128]{3,1,0,2:T(4,128)}), f32[2,4,128,128]{3,1,0,2:T(4,128)S(1)}, u32[]{:S(2)}, u32[]{:S(2)}) async-start(f32[2,4,128,128]{3,1,0,2:T(4,128)} %copy.91), calls=%async_computation | async-start | bytes 1048576 | tf_op jit(solution)/shard_map/all_to_all | solution.py:70
  63.4 27.7 %all-to-all-start.2 = ((f32[2,4,128,128]{2,1,0,3:T(4,128)}), f32[2,4,128,128]{2,1,0,3:T(4,128)S(1)}, u32[]{:S(2)}, u32[]{:S(2)}) async-start(f32[2,4,128,128]{2,1,0,3:T(4,128)} %copy.99), calls=%async_computation.2 | async-start | bytes 1048576 | tf_op jit(solution)/shard_map/all_to_all | solution.py:73
  94.0 18.8 %all-to-all-start.3 = ((f32[2,32,128,16]{2,3,0,1:T(8,128)}), f32[2,32,128,16]{2,3,0,1:T(8,128)S(1)}, u32[]{:S(2)}, u32[]{:S(2)}) async-start(f32[2,32,128,16]{2,3,0,1:T(8,128)} %copy.106), calls=%async_computation.3 | async-start | bytes 1048576 | tf_op jit(solution)/shard_map/all_to_all | solution.py:76
  101.4 11.7 %copy-start = (f32[4,128,128]{2,1,0:T(8,128)S(1)}, f32[4,128,128]{2,1,0:T(8,128)}, u32[]{:S(2)}) copy-start(f32[4,128,128]{2,1,0:T(8,128)} %param.5) | copy-start | bytes 786436
  119.1 20.2 %all-to-all-start.4 = ((f32[2,4,128,128]{3,1,0,2:T(4,128)}), f32[2,4,128,128]{3,1,0,2:T(4,128)S(1)}, u32[]{:S(2)}, u32[]{:S(2)}) async-start(f32[2,4,128,128]{3,1,0,2:T(4,128)} %copy.116), calls=%async_computation.4 | async-start | bytes 1048576 | tf_op jit(solution)/shard_map/all_to_all | solution.py:70
  163.8 21.4 %all-to-all-start.6 = ((f32[2,4,128,128]{2,1,0,3:T(4,128)}), f32[2,4,128,128]{2,1,0,3:T(4,128)S(1)}, u32[]{:S(2)}, u32[]{:S(2)}) async-start(f32[2,4,128,128]{2,1,0,3:T(4,128)} %copy.124), calls=%async_computation.6 | async-start | bytes 1048576 | tf_op jit(solution)/shard_map/all_to_all | solution.py:73
  207.1 18.4 %all-to-all-start.8 = ((f32[32,4,4,128]{3,2,1,0:T(4,128)}), f32[32,4,4,128]{3,2,1,0:T(4,128)S(1)}, u32[]{:S(2)}, u32[]{:S(2)}) async-start(f32[32,4,4,128]{3,2,1,0:T(4,128)} %copy.135), calls=%async_computation.8 | async-start | bytes 524288 | tf_op jit(solution)/shard_map/all_to_all | solution.py:17
where the time goes:
time: 228 us; the launch traced here: 226 us
  waiting for transfers between devices  75.8 us (33%)
  blocking collectives  55.2 us (24%)
  starting transfers between devices  49.5 us (22%)
  matrix products  15.4 us (7%)
  local copies, waits for them, and re-layouts  13.3 us (6%)
  between operations  12.4 us (5%)
  other arithmetic  4.54 us (2%)
    all_to_all x2, blocking collectives, on_device(): lax.all_to_all(moved, 'bank', split_axis=1, concat_axis=2, tiled=True)  37.5 us
    all_to_all x2, waiting for transfers between devices, on_device(): lax.all_to_all(values, 'bank', split_axis=2, concat_axis=1, tiled=True)  27.6 us
    all_to_all x2, waiting for transfers between devices, on_device(): lax.all_to_all(values, 'lane', split_axis=3, concat_axis=1, tiled=True)  26 us
    all_to_all x2, starting transfers between devices, on_device(): lax.all_to_all(values, 'lane', split_axis=3, concat_axis=1, tiled=True)  20.3 us
    all_to_all x2, starting transfers between devices, on_device(): lax.all_to_all(values, 'bank', split_axis=2, concat_axis=1, tiled=True)  18.4 us
    all_to_all x1, blocking collectives, on_device(): lax.all_to_all(moved, 'lane', split_axis=1, concat_axis=3, tiled=True)  17.7 us
    dot_general x16, matrix products, times(): jnp.tensordot(values, table, axes=([dim], [0]), precision=lax.Precision.H...  15.4 us
    all_to_all x1, waiting for transfers between devices, on_device(): lax.all_to_all(moved, 'lane', split_axis=1, concat_axis=3, tiled=True)  11.3 us
  transfers between devices with their start and end apart: 6, of which 6 were waited for; matrix products, arithmetic and copies ran while one was open for 0% of the time, Pallas kernels for 0%

commit v1 on v0

v1 whole, which is shorter than its diff:
```python
import jax
import jax.numpy as jnp
from jax import lax
from jax.experimental import pallas as pl
from jax.experimental.pallas import tpu as pltpu
from jax.sharding import PartitionSpec as P


ROT, ROT_T, FLIP = 0, 1, 2
GROUP = ("lane", "bank")


def trig(x):
    y = x * x
    c = jnp.full_like(x, 1.0 / 20922789888000.0)
    s = jnp.full_like(x, 1.0 / 355687428096000.0)
    for k in (-87178291200.0, 479001600.0, -3628800.0, 40320.0, -720.0, 24.0, -2.0, 1.0):
        c = c * y + 1.0 / k
    for k in (-1307674368000.0, 6227020800.0, -39916800.0, 362880.0, -5040.0, 120.0, -6.0, 1.0):
        s = s * y + 1.0 / k
    return c, s * x


def angle(mix_ref, layer, group, width=128):
    return trig(jnp.full((1, width), mix_ref[layer, group], jnp.float32))


def iota(shape, dim):
    return lax.broadcasted_iota(jnp.int32, shape, dim)


def bit(value, k):
    return (value >> k) & 1


def pop(value, bits):
    total = bit(value, 0)
    for k in range(1, bits):
        total = total + bit(value, k)
    return total


def pair(kind, c, s):
    if kind == ROT:
        return c, s, -s, c
    if kind == ROT_T:
        return c, -s, s, c
    return c, s, s, -c


def table(shape, pairs):
    i, j = iota(shape, 0), iota(shape, 1)
    out = None
    for ki, kj, kind, c, s in pairs:
        a00, a01, a10, a11 = pair(kind, c, s)
        odd = bit(j, kj) == 1
        part = jnp.where(bit(i, ki) == 1, jnp.where(odd, a11, a10), jnp.where(odd, a01, a00))
        out = part if out is None else out * part
    return out


def doubled(small, kind, c, s):
    a00, a01, a10, a11 = pair(kind, c, s)
    top = jnp.concatenate([small * a00, small * a01], axis=1)
    low = jnp.concatenate([small * a10, small * a11], axis=1)
    return jnp.concatenate([top, low], axis=0)


def halves(x):
    high = x.astype(jnp.bfloat16)
    return high, (x - high.astype(jnp.float32)).astype(jnp.bfloat16)


def mm(a, b):
    ah, al = halves(a)
    bh, bl = halves(b)

    def one(p, q):
        return jnp.dot(p, q, preferred_element_type=jnp.float32)

    return one(ah, bh) + (one(ah, bl) + one(al, bh))


def own_pop():
    return pop(lax.axis_index("bank"), 5) + pop(lax.axis_index("lane"), 3)


def quarter_turns(extra):
    shape = (128, 128)
    p = pop(iota(shape, 0), 7) + pop(iota(shape, 1), 7) + extra
    return bit(p, 0) == 1, 1.0 - 2.0 * bit(p, 1).astype(jnp.float32)


def first_kernel(amp, en, ph, mix, out):
    own = own_pop()
    turns = [quarter_turns(own + k) for k in range(3)]
    xr, xi = [], []
    for t in range(4):
        odd, sign = turns[bin(t).count("1")]
        e = en[t]
        c, s = trig(ph[0:1, :] * e)
        c, s = jnp.where(odd, -s, c) * sign, jnp.where(odd, c, s) * sign
        re, im = amp[0, t], amp[1, t]
        xr.append(re * c + im * s)
        xi.append(im * c - re * s)
        e2 = (ph[1:2, :] * e).T
        for lb in range(2):
            out[pl.ds(t * 64 * 6 + 4 + lb, 64, stride=6), :] = e2[lb * 64 : lb * 64 + 64]
    c, s = angle(mix, 0, 2)
    x = []
    for v in (xr, xi):
        v = [c * v[0] + s * v[1], c * v[1] - s * v[0], c * v[2] + s * v[3], c * v[3] - s * v[2]]
        x += [c * v[0] + s * v[2], c * v[1] + s * v[3], c * v[2] - s * v[0], c * v[3] - s * v[1]]
    c, s = angle(mix, 0, 0)
    lanes = table((128, 128), [(k, k, ROT_T, c, s) for k in range(7)])
    c, s = angle(mix, 0, 1)
    rows = table((128, 128), [(k, k, ROT_T, c, s) for k in range(7)])
    y = mm(jnp.concatenate(x, axis=0), lanes)
    y = jnp.concatenate([y[k * 128 : k * 128 + 128].T for k in range(8)], axis=0)
    y = mm(y, rows)
    for c in range(2):
        for t in range(4):
            for lb in range(2):
                at = (c * 4 + t) * 128 + lb * 64
                out[pl.ds(t * 64 * 6 + c * 2 + lb, 64, stride=6), :] = y[at : at + 64]


def device_bits(mix, layer, kind):
    c2, s2 = angle(mix, layer, 2)
    c3, s3 = angle(mix, layer, 3)
    small = table(
        (128, 128), [(k, k, kind, c2, s2) for k in range(5)] + [(k, k, kind, c3, s3) for k in (5, 6)]
    )
    return doubled(small, kind, c3, s3)


def second_kernel(arrived, mix, out):
    x = jnp.concatenate([arrived[pl.ds(k, 256, stride=6), :] for k in range(4)], axis=1)
    y = mm(device_bits(mix, 0, ROT), x)
    z = [None] * 4
    for lb in range(2):
        c, s = trig(arrived[pl.ds(4 + lb, 256, stride=6), :])
        re, im = y[:, lb * 128 : lb * 128 + 128], y[:, 256 + lb * 128 : 384 + lb * 128]
        z[lb] = re * c + im * s
        z[2 + lb] = im * c - re * s
    c1, s1 = angle(mix, 1, 1)
    moved = (5, 6, 0, 1, 2, 3, 4)
    rows = table((128, 128), [(k, moved[k], FLIP, c1, s1) for k in range(7)])
    c0, s0 = angle(mix, 1, 0)
    z = jnp.concatenate(
        [jnp.concatenate(z[:2], axis=1), jnp.concatenate(z[2:], axis=1)], axis=0
    )
    z = mm(z, doubled(rows, FLIP, c0, s0))
    v = mm(device_bits(mix, 1, FLIP), jnp.concatenate([z[:256], z[256:]], axis=1))
    v = [v[:, k * 128 : k * 128 + 128] for k in range(4)]
    for k in range(4):
        out[pl.ds(k, 256, stride=8), :] = v[k]
    lane = iota((128, 128), 1)
    upper, third = lane >= 64, bit(lane, 5) == 1
    for h in range(2):
        a = [v[k][h * 128 : h * 128 + 128].T for k in range(4)]
        a = [
            jnp.where(upper, pltpu.roll(a[2], 64, 1), a[0]),
            jnp.where(upper, pltpu.roll(a[3], 64, 1), a[1]),
            jnp.where(upper, a[2], pltpu.roll(a[0], 64, 1)),
            jnp.where(upper, a[3], pltpu.roll(a[1], 64, 1)),
        ]
        for k in (0, 2):
            low, high = a[k], a[k + 1]
            a[k] = jnp.where(third, pltpu.roll(high, 32, 1), low)
            a[k + 1] = jnp.where(third, high, pltpu.roll(low, 96, 1))
        for m in range(4):
            for q in range(4):
                at = (h * 4 + m) * 256 + 4 + q
                out[pl.ds(at, 32, stride=8), :] = a[m][q * 32 : q * 32 + 32]


def third_kernel(arrived, mix, final, marginal):
    c0, s0 = angle(mix, 1, 0)
    c2, s2 = angle(mix, 1, 2)
    small = table(
        (128, 128), [(k, k, FLIP, c0, s0) for k in range(6)] + [(6, 6, FLIP, c2, s2)]
    )
    w = doubled(small, FLIP, c2, s2)
    x = jnp.concatenate([arrived[pl.ds(k, 256, stride=8), :] for k in range(8)], axis=1)
    y = mm(w, x)
    own = own_pop()
    turns = [quarter_turns(own + k) for k in range(3)]
    for t in range(4):
        odd, sign = turns[bin(t).count("1")]
        f = []
        for c in range(2):
            part = [y[t * 64 : t * 64 + 64, (c * 2 + lb) * 128 : (c * 2 + lb) * 128 + 128] for lb in range(2)]
            f.append(jnp.concatenate(part, axis=0).T)
        re, im = jnp.where(odd, f[1], f[0]) * sign, jnp.where(odd, -f[0], f[1]) * sign
        for q in range(4):
            final[0, t, pl.ds(q, 32, stride=4), :] = re[q * 32 : q * 32 + 32]
            final[1, t, pl.ds(q, 32, stride=4), :] = im[q * 32 : q * 32 + 32]
    for q in range(4):
        chance = y[:, (4 + q) * 128 : (5 + q) * 128]
        chance = chance * chance
        chance = chance + pltpu.roll(chance, 64, 1)
        for t in range(4):
            turned = jnp.concatenate([chance[t * 64 : t * 64 + 64], chance[t * 64 : t * 64 + 64]], axis=0).T
            low = jnp.sum(turned[0:32], axis=0, keepdims=True)
            high = jnp.sum(turned[32:64], axis=0, keepdims=True)
            marginal[t, q : q + 1, :] = jnp.where(iota((1, 128), 1) >= 64, high, low) * (1.0 / 32.0)


def full(shape):
    return pl.BlockSpec(shape, lambda: (0,) * len(shape))


def call(body, outs, *args):
    specs = [
        pl.BlockSpec(memory_space=pltpu.SMEM) if a.shape == (2, 4) else full(a.shape) for a in args
    ]
    return pl.pallas_call(
        body,
        out_shape=[jax.ShapeDtypeStruct(s, jnp.float32) for s in outs],
        in_specs=specs,
        out_specs=[full(s) for s in outs],
    )(*args)


def exchange(values, *chunk):
    moved = lax.all_to_all(values.reshape(256, *chunk), GROUP, 0, 0, tiled=True)
    return moved.reshape(values.shape)


def on_device(amplitudes, energies, phase_angles, mix_angles):
    (sent,) = call(first_kernel, [(1536, 128)], amplitudes, energies, phase_angles, mix_angles)
    arrived = exchange(sent, 3, 2, 128)
    (sent,) = call(second_kernel, [(2048, 128)], arrived, mix_angles)
    arrived = exchange(sent, 8, 128)
    final, marginal = call(
        third_kernel, [(2, 4, 128, 128), (4, 4, 128)], arrived, mix_angles
    )
    return final, marginal


def solution(mesh):
    placed = (P(None, ("bank", "lane"), None, None), P(("bank", "lane"), None, None), P(), P())
    return jax.shard_map(
        on_device,
        mesh=mesh,
        in_specs=placed,
        out_specs=(P(None, ("bank", "lane"), None, None), P("lane", "bank", None)),
        check_vma=False,
    )
```

time: 228 us -> 92.1 us (0.40)
  waiting for transfers between devices: 75.8 us -> 0 us
  starting transfers between devices: 49.5 us -> 0 us
  blocking collectives: 55.2 us -> 80.1 us
  matrix products: 15.4 us -> 0 us
  local copies, waits for them, and re-layouts: 13.3 us -> 0 us
  between operations: 12.4 us -> 0.63 us
  Pallas kernels: 0 us -> 11.1 us
  other arithmetic: 4.54 us -> 0 us
    all_to_all x6 -> x0, waiting for transfers between devices: 75.8 us -> none  [the longest x2 27.6 us: on_device(): lax.all_to_all(values, 'bank', split_axis=2, concat_axis=1, tiled=True)]
    all_to_all x6 -> x0, starting transfers between devices: 49.5 us -> none  [the longest x2 20.3 us: on_device(): lax.all_to_all(values, 'lane', split_axis=3, concat_axis=1, tiled=True)]
    all_to_all x3 -> x2, blocking collectives: 55.2 us -> 80.1 us  [exchange(): moved = lax.all_to_all(values.reshape(256, *chunk), GROUP, 0, 0, tiled=True)]
    dot_general x16 -> x0, matrix products: 15.4 us -> none  [times(): jnp.tensordot(values, table, axes=([dim], [0]), precision=lax.Precision.H...]
    pallas_call x0 -> x3, Pallas kernels: none -> 11.1 us  [call(): pl.pallas_call(body, out_shape=[jax.ShapeDtypeStruct(s, jnp.float32) for...]
    all_to_all x13 -> x0, local copies, waits for them, and re-layouts: 3.87 us -> none  [the longest x6 2.88 us: on_device(): lax.all_to_all(moved, 'bank', split_axis=1, concat_axis=2, tiled=True)]
    another operation x6 -> x0, local copies, waits for them, and re-layouts: 3.42 us -> none  [apply_along(): return jnp.stack([by_real[0] - by_imag[1], by_real[1] + by_imag[0]])]
    another operation x8 -> x0, other arithmetic: 3.3 us -> none  [the longest x2 3.08 us: diagonal_step(): jnp.stack([values[0] * jnp.cos(turn) + values[1] * jnp.sin(turn), values[...]
  transfers between devices with their start and end apart: 6 -> 0, of which waited for: 6 -> 0; matrix products, arithmetic and copies ran while one was open for 0% -> 0% of each run, Pallas kernels for 0% -> 0%
where the time goes in v1:
time: 92.1 us; the launch traced here: 91.8 us
  blocking collectives  80.1 us (87%)
  Pallas kernels  11.1 us (12%)
    all_to_all x2, blocking collectives, exchange(): moved = lax.all_to_all(values.reshape(256, *chunk), GROUP, 0, 0, tiled=True)  80.1 us
    pallas_call x3, Pallas kernels, call(): pl.pallas_call(body, out_shape=[jax.ShapeDtypeStruct(s, jnp.float32) for...  11.1 us

profile of v1, /device:TPU:1, one launch (start us, length us, event | category | flops | bytes accessed | tf_op | source)
XLA Modules:
  0.0 91.8 jit_solution(16539185354938841995)
XLA Ops:
  0.6 3.7 %shard_map.59 = f32[1536,128]{1,0:T(8,128)} custom-call(f32[2,4,128,128]{3,2,1,0:T(8,128)} %amp.1, f32[4,128,128]{2,1,0:T(8,128)} %en.1, f32[2,128]{1,0:T(2,128)} %ph.1, f32[2,4]{1,0:T(2,128)} %mix.5), custom_call_target="tpu_custom_call" | custom-call | tf_op jit(solution)/shard_map/pallas_call | solution.py:218
  4.3 42.3 %all_to_all.10 = f32[256,3,2,128]{3,2,1,0:T(2,128)} all-to-all(f32[256,3,2,128]{3,2,1,0:T(2,128)} %bitcast.7), channel_id=1, replica_groups=mesh['bank'=32,'lane'=8] {'lane','bank'}, dimensions={0} | all-to-all | bytes 1572864 | tf_op jit(solution)/shard_map/all_to_all | solution.py:227
  46.6 4.3 %shard_map.60 = f32[2048,128]{1,0:T(8,128)} custom-call(f32[1536,128]{1,0:T(8,128)} %bitcast.6, f32[2,4]{1,0:T(2,128)} %mix.5), custom_call_target="tpu_custom_call" | custom-call | tf_op jit(solution)/shard_map/pallas_call | solution.py:218
  50.8 37.8 %all_to_all.11 = f32[256,8,128]{2,1,0:T(8,128)} all-to-all(f32[256,8,128]{2,1,0:T(8,128)} %bitcast.5), channel_id=1, replica_groups=mesh['bank'=32,'lane'=8] {'lane','bank'}, dimensions={0} | all-to-all | bytes 2097152 | tf_op jit(solution)/shard_map/all_to_all | solution.py:227
  88.7 3.2 %shard_map.61 = (f32[2,4,128,128]{3,2,1,0:T(8,128)}, f32[4,4,128]{2,1,0:T(4,128)}) custom-call(f32[2048,128]{1,0:T(8,128)} %bitcast.4, f32[2,4]{1,0:T(2,128)} %mix.5), custom_call_target="tpu_custom_call" | custom-call | tf_op jit(solution)/shard_map/pallas_call | solution.py:218

commit v2 on v1

--- a/solution.py
+++ b/solution.py
@@ -211,27 +211,31 @@
     return pl.BlockSpec(shape, lambda: (0,) * len(shape))
 
 
-def call(body, outs, *args):
+def call(body, outs, *args, inner=False):
     specs = [
-        pl.BlockSpec(memory_space=pltpu.SMEM) if a.shape == (2, 4) else full(a.shape) for a in args
+        pl.BlockSpec(memory_space=pltpu.SMEM) if a.shape == (2, 4) else pl.BlockSpec(memory_space=pltpu.VMEM) if a.shape[0] > 1000 else full(a.shape) for a in args
     ]
     return pl.pallas_call(
         body,
-        out_shape=[jax.ShapeDtypeStruct(s, jnp.float32) for s in outs],
+        out_shape=[
+            pltpu.VMEM(s, jnp.float32) if inner else jax.ShapeDtypeStruct(s, jnp.float32) for s in outs
+        ],
         in_specs=specs,
-        out_specs=[full(s) for s in outs],
+        out_specs=[
+            pl.BlockSpec(memory_space=pltpu.VMEM) if inner else full(s) for s in outs
+        ],
     )(*args)
 
 
 def exchange(values, *chunk):
     moved = lax.all_to_all(values.reshape(256, *chunk), GROUP, 0, 0, tiled=True)
-    return moved.reshape(values.shape)
+    return pltpu.with_memory_space_constraint(moved.reshape(values.shape), pltpu.VMEM)
 
 
 def on_device(amplitudes, energies, phase_angles, mix_angles):
-    (sent,) = call(first_kernel, [(1536, 128)], amplitudes, energies, phase_angles, mix_angles)
+    (sent,) = call(first_kernel, [(1536, 128)], amplitudes, energies, phase_angles, mix_angles, inner=True)
     arrived = exchange(sent, 3, 2, 128)
-    (sent,) = call(second_kernel, [(2048, 128)], arrived, mix_angles)
+    (sent,) = call(second_kernel, [(2048, 128)], arrived, mix_angles, inner=True)
     arrived = exchange(sent, 8, 128)
     final, marginal = call(
         third_kernel, [(2, 4, 128, 128), (4, 4, 128)], arrived, mix_angles

time: 92.1 us -> 87.8 us (0.953)
  Pallas kernels: 11.1 us -> 8.21 us
  blocking collectives: 80.1 us -> 78.7 us
    pallas_call x3, Pallas kernels: 11.1 us -> 8.21 us  [call(): pl.pallas_call(body, out_shape=[pltpu.VMEM(s, jnp.float32) if inner else...]
    all_to_all x2, blocking collectives: 80.1 us -> 78.7 us  [exchange(): moved = lax.all_to_all(values.reshape(256, *chunk), GROUP, 0, 0, tiled=True)]
where the time goes in v2:
time: 87.8 us; the launch traced here: 87.6 us
  blocking collectives  78.7 us (90%)
  Pallas kernels  8.21 us (9%)
    all_to_all x2, blocking collectives, exchange(): moved = lax.all_to_all(values.reshape(256, *chunk), GROUP, 0, 0, tiled=True)  78.7 us
    pallas_call x3, Pallas kernels, call(): pl.pallas_call(body, out_shape=[pltpu.VMEM(s, jnp.float32) if inner else...  8.21 us

profile of v2, /device:TPU:1, one launch (start us, length us, event | category | flops | bytes accessed | tf_op | source)
XLA Modules:
  0.0 87.6 jit_solution(16693577703914650449)
XLA Ops:
  0.6 2.8 %shard_map.59 = f32[1536,128]{1,0:T(8,128)S(1)} custom-call(f32[2,4,128,128]{3,2,1,0:T(8,128)} %amp.1, f32[4,128,128]{2,1,0:T(8,128)} %en.1, f32[2,128]{1,0:T(2,128)} %ph.1, f32[2,4]{1,0:T(2,128)} %mix.5), custom_call_target="tpu_custom_call" | custom-call | tf_op jit(solution)/shard_map/pallas_call | solution.py:218
  3.4 42.0 %all_to_all.10 = f32[256,3,2,128]{3,2,1,0:T(2,128)S(1)} all-to-all(f32[256,3,2,128]{3,2,1,0:T(2,128)S(1)} %bitcast.7), channel_id=1, replica_groups=mesh['bank'=32,'lane'=8] {'lane','bank'}, dimensions={0} | all-to-all | bytes 1572864 | tf_op jit(solution)/shard_map/all_to_all | solution.py:231
  45.4 2.8 %shard_map.60 = f32[2048,128]{1,0:T(8,128)S(1)} custom-call(f32[1536,128]{1,0:T(8,128)S(1)} %bitcast.6, f32[2,4]{1,0:T(2,128)} %mix.5), custom_call_target="tpu_custom_call" | custom-call | tf_op jit(solution)/shard_map/pallas_call | solution.py:218
  48.2 36.8 %all_to_all.11 = f32[256,8,128]{2,1,0:T(8,128)S(1)} all-to-all(f32[256,8,128]{2,1,0:T(8,128)S(1)} %bitcast.5), channel_id=1, replica_groups=mesh['bank'=32,'lane'=8] {'lane','bank'}, dimensions={0} | all-to-all | bytes 2097152 | tf_op jit(solution)/shard_map/all_to_all | solution.py:231
  85.0 2.6 %shard_map.61 = (f32[2,4,128,128]{3,2,1,0:T(8,128)}, f32[4,4,128]{2,1,0:T(4,128)}) custom-call(f32[2048,128]{1,0:T(8,128)S(1)} %bitcast.4, f32[2,4]{1,0:T(2,128)} %mix.5), custom_call_target="tpu_custom_call" | custom-call | tf_op jit(solution)/shard_map/pallas_call | solution.py:218

commit v3 on v2

--- a/solution.py
+++ b/solution.py
@@ -11,14 +11,17 @@
 
 
 def trig(x):
-    y = x * x
-    c = jnp.full_like(x, 1.0 / 20922789888000.0)
-    s = jnp.full_like(x, 1.0 / 355687428096000.0)
-    for k in (-87178291200.0, 479001600.0, -3628800.0, 40320.0, -720.0, 24.0, -2.0, 1.0):
+    h = x * 0.5
+    y = h * h
+    c = jnp.full_like(x, 1.0 / 479001600.0)
+    s = jnp.full_like(x, 1.0 / 6227020800.0)
+    for k in (-3628800.0, 40320.0, -720.0, 24.0, -2.0):
         c = c * y + 1.0 / k
-    for k in (-1307674368000.0, 6227020800.0, -39916800.0, 362880.0, -5040.0, 120.0, -6.0, 1.0):
+    for k in (-39916800.0, 362880.0, -5040.0, 120.0, -6.0, 1.0):
         s = s * y + 1.0 / k
-    return c, s * x
+    s = s * h
+    c = c * y
+    return 1.0 - 2.0 * s * s, 2.0 * s + 2.0 * s * c
 
 
 def angle(mix_ref, layer, group, width=128):
@@ -48,14 +51,18 @@
     return c, s, s, -c
 
 
-def table(shape, pairs):
-    i, j = iota(shape, 0), iota(shape, 1)
-    out = None
-    for ki, kj, kind, c, s in pairs:
+def table(pairs):
+    j = iota((1, 128), 1)
+    i = iota((8, 1), 0)
+    out = jnp.ones((8, 128), jnp.float32)
+    for k, kj, kind, c, s in pairs:
         a00, a01, a10, a11 = pair(kind, c, s)
         odd = bit(j, kj) == 1
-        part = jnp.where(bit(i, ki) == 1, jnp.where(odd, a11, a10), jnp.where(odd, a01, a00))
-        out = part if out is None else out * part
+        upper, lower = jnp.where(odd, a01, a00), jnp.where(odd, a11, a10)
+        if k < 3:
+            out = out * jnp.where(bit(i, k) == 1, lower, upper)
+        else:
+            out = jnp.concatenate([out * upper, out * lower], axis=0)
     return out
 
 
@@ -74,11 +81,11 @@
 def mm(a, b):
     ah, al = halves(a)
     bh, bl = halves(b)
-
-    def one(p, q):
-        return jnp.dot(p, q, preferred_element_type=jnp.float32)
-
-    return one(ah, bh) + (one(ah, bl) + one(al, bh))
+    return jnp.dot(
+        jnp.concatenate([ah, ah, al], axis=1),
+        jnp.concatenate([bh, bl, bh], axis=0),
+        preferred_element_type=jnp.float32,
+    )
 
 
 def own_pop():
@@ -106,31 +113,34 @@
         e2 = (ph[1:2, :] * e).T
         for lb in range(2):
             out[pl.ds(t * 64 * 6 + 4 + lb, 64, stride=6), :] = e2[lb * 64 : lb * 64 + 64]
-    c, s = angle(mix, 0, 2)
-    x = []
-    for v in (xr, xi):
-        v = [c * v[0] + s * v[1], c * v[1] - s * v[0], c * v[2] + s * v[3], c * v[3] - s * v[2]]
-        x += [c * v[0] + s * v[2], c * v[1] + s * v[3], c * v[2] - s * v[0], c * v[3] - s * v[1]]
+    bits = range(7)
+    c2, s2 = angle(mix, 0, 2)
     c, s = angle(mix, 0, 0)
-    lanes = table((128, 128), [(k, k, ROT_T, c, s) for k in range(7)])
+    lanes = doubled(table([(k, k, ROT_T, c, s) for k in bits]), ROT_T, c2, s2)
     c, s = angle(mix, 0, 1)
-    rows = table((128, 128), [(k, k, ROT_T, c, s) for k in range(7)])
+    rows = doubled(table([(k, k, ROT_T, c, s) for k in bits]), ROT_T, c2, s2)
+    x = [jnp.concatenate([v[t], v[t + 1]], axis=1) for v in (xr, xi) for t in (0, 2)]
     y = mm(jnp.concatenate(x, axis=0), lanes)
-    y = jnp.concatenate([y[k * 128 : k * 128 + 128].T for k in range(8)], axis=0)
-    y = mm(y, rows)
+    z = []
+    for c in range(2):
+        for low in range(2):
+            part = [
+                y[(c * 2 + high) * 128 : (c * 2 + high) * 128 + 128, low * 128 : low * 128 + 128].T
+                for high in range(2)
+            ]
+            z.append(jnp.concatenate(part, axis=1))
+    y = mm(jnp.concatenate(z, axis=0), rows)
     for c in range(2):
         for t in range(4):
             for lb in range(2):
-                at = (c * 4 + t) * 128 + lb * 64
-                out[pl.ds(t * 64 * 6 + c * 2 + lb, 64, stride=6), :] = y[at : at + 64]
+                at = (c * 2 + t % 2) * 128 + lb * 64
+                out[pl.ds(t * 64 * 6 + c * 2 + lb, 64, stride=6), :] = y[at : at + 64, t // 2 * 128 : t // 2 * 128 + 128]
 
 
 def device_bits(mix, layer, kind):
     c2, s2 = angle(mix, layer, 2)
     c3, s3 = angle(mix, layer, 3)
-    small = table(
-        (128, 128), [(k, k, kind, c2, s2) for k in range(5)] + [(k, k, kind, c3, s3) for k in (5, 6)]
-    )
+    small = table([(k, k, kind, c2, s2) for k in range(5)] + [(k, k, kind, c3, s3) for k in (5, 6)])
     return doubled(small, kind, c3, s3)
 
 
@@ -145,7 +155,7 @@
         z[2 + lb] = im * c - re * s
     c1, s1 = angle(mix, 1, 1)
     moved = (5, 6, 0, 1, 2, 3, 4)
-    rows = table((128, 128), [(k, moved[k], FLIP, c1, s1) for k in range(7)])
+    rows = table([(k, moved[k], FLIP, c1, s1) for k in range(7)])
     c0, s0 = angle(mix, 1, 0)
     z = jnp.concatenate(
         [jnp.concatenate(z[:2], axis=1), jnp.concatenate(z[2:], axis=1)], axis=0
@@ -155,32 +165,16 @@
     v = [v[:, k * 128 : k * 128 + 128] for k in range(4)]
     for k in range(4):
         out[pl.ds(k, 256, stride=8), :] = v[k]
-    lane = iota((128, 128), 1)
-    upper, third = lane >= 64, bit(lane, 5) == 1
-    for h in range(2):
-        a = [v[k][h * 128 : h * 128 + 128].T for k in range(4)]
-        a = [
-            jnp.where(upper, pltpu.roll(a[2], 64, 1), a[0]),
-            jnp.where(upper, pltpu.roll(a[3], 64, 1), a[1]),
-            jnp.where(upper, a[2], pltpu.roll(a[0], 64, 1)),
-            jnp.where(upper, a[3], pltpu.roll(a[1], 64, 1)),
-        ]
-        for k in (0, 2):
-            low, high = a[k], a[k + 1]
-            a[k] = jnp.where(third, pltpu.roll(high, 32, 1), low)
-            a[k + 1] = jnp.where(third, high, pltpu.roll(low, 96, 1))
-        for m in range(4):
-            for q in range(4):
-                at = (h * 4 + m) * 256 + 4 + q
-                out[pl.ds(at, 32, stride=8), :] = a[m][q * 32 : q * 32 + 32]
+    for m in range(8):
+        a = jnp.concatenate([v[k][m * 32 : m * 32 + 32] for k in range(4)], axis=0).T
+        for q in range(4):
+            out[pl.ds(m * 256 + 4 + q, 32, stride=8), :] = a[q * 32 : q * 32 + 32]
 
 
 def third_kernel(arrived, mix, final, marginal):
     c0, s0 = angle(mix, 1, 0)
     c2, s2 = angle(mix, 1, 2)
-    small = table(
-        (128, 128), [(k, k, FLIP, c0, s0) for k in range(6)] + [(6, 6, FLIP, c2, s2)]
-    )
+    small = table([(k, k, FLIP, c0, s0) for k in range(6)] + [(6, 6, FLIP, c2, s2)])
     w = doubled(small, FLIP, c2, s2)
     x = jnp.concatenate([arrived[pl.ds(k, 256, stride=8), :] for k in range(8)], axis=1)
     y = mm(w, x)
@@ -196,15 +190,22 @@
         for q in range(4):
             final[0, t, pl.ds(q, 32, stride=4), :] = re[q * 32 : q * 32 + 32]
             final[1, t, pl.ds(q, 32, stride=4), :] = im[q * 32 : q * 32 + 32]
+    pick = jnp.where(bit(iota((8, 128), 1), 5) == iota((8, 128), 0), 1.0 / 32.0, 0.0).astype(jnp.bfloat16)
+    upper = iota((1, 128), 1) >= 64
     for q in range(4):
         chance = y[:, (4 + q) * 128 : (5 + q) * 128]
-        chance = chance * chance
-        chance = chance + pltpu.roll(chance, 64, 1)
+        high, low = halves(chance * chance)
+        total = lax.dot_general(
+            jnp.concatenate([pick, pick], axis=1),
+            jnp.concatenate([high, low], axis=1),
+            (((1,), (1,)), ((), ())),
+            preferred_element_type=jnp.float32,
+        )
         for t in range(4):
-            turned = jnp.concatenate([chance[t * 64 : t * 64 + 64], chance[t * 64 : t * 64 + 64]], axis=0).T
-            low = jnp.sum(turned[0:32], axis=0, keepdims=True)
-            high = jnp.sum(turned[32:64], axis=0, keepdims=True)
-            marginal[t, q : q + 1, :] = jnp.where(iota((1, 128), 1) >= 64, high, low) * (1.0 / 32.0)
+            part = total[:, t // 2 * 128 : t // 2 * 128 + 128]
+            moved = pltpu.roll(part, 64, 1)
+            first, second = (moved, part) if t % 2 else (part, moved)
+            marginal[t, q : q + 1, :] = jnp.where(upper, second[1:2], first[0:1])
 
 
 def full(shape):

time: 87.8 us -> 86.8 us (0.989)
  Pallas kernels: 8.21 us -> 7.28 us
    pallas_call x3, Pallas kernels: 8.21 us -> 7.28 us  [call(): pl.pallas_call(body, out_shape=[pltpu.VMEM(s, jnp.float32) if inner else...]
where the time goes in v3:
time: 86.8 us; the launch traced here: 86.6 us
  blocking collectives  78.7 us (91%)
  Pallas kernels  7.28 us (8%)
    all_to_all x2, blocking collectives, exchange(): moved = lax.all_to_all(values.reshape(256, *chunk), GROUP, 0, 0, tiled=True)  78.7 us
    pallas_call x3, Pallas kernels, call(): pl.pallas_call(body, out_shape=[pltpu.VMEM(s, jnp.float32) if inner else...  7.28 us

profile of v3, /device:TPU:1, one launch (start us, length us, event | category | flops | bytes accessed | tf_op | source)
XLA Modules:
  0.0 86.6 jit_solution(598808098876509399)
XLA Ops:
  0.6 2.6 %shard_map.59 = f32[1536,128]{1,0:T(8,128)S(1)} custom-call(f32[2,4,128,128]{3,2,1,0:T(8,128)} %amp.1, f32[4,128,128]{2,1,0:T(8,128)} %en.1, f32[2,128]{1,0:T(2,128)} %ph.1, f32[2,4]{1,0:T(2,128)} %mix.5), custom_call_target="tpu_custom_call" | custom-call | tf_op jit(solution)/shard_map/pallas_call | solution.py:219
  3.2 42.0 %all_to_all.10 = f32[256,3,2,128]{3,2,1,0:T(2,128)S(1)} all-to-all(f32[256,3,2,128]{3,2,1,0:T(2,128)S(1)} %bitcast.7), channel_id=1, replica_groups=mesh['bank'=32,'lane'=8] {'lane','bank'}, dimensions={0} | all-to-all | bytes 1572864 | tf_op jit(solution)/shard_map/all_to_all | solution.py:232
  45.2 2.3 %shard_map.60 = f32[2048,128]{1,0:T(8,128)S(1)} custom-call(f32[1536,128]{1,0:T(8,128)S(1)} %bitcast.6, f32[2,4]{1,0:T(2,128)} %mix.5), custom_call_target="tpu_custom_call" | custom-call | tf_op jit(solution)/shard_map/pallas_call | solution.py:219
  47.5 36.8 %all_to_all.11 = f32[256,8,128]{2,1,0:T(8,128)S(1)} all-to-all(f32[256,8,128]{2,1,0:T(8,128)S(1)} %bitcast.5), channel_id=1, replica_groups=mesh['bank'=32,'lane'=8] {'lane','bank'}, dimensions={0} | all-to-all | bytes 2097152 | tf_op jit(solution)/shard_map/all_to_all | solution.py:232
  84.3 2.4 %shard_map.61 = (f32[2,4,128,128]{3,2,1,0:T(8,128)}, f32[4,4,128]{2,1,0:T(4,128)}) custom-call(f32[2048,128]{1,0:T(8,128)S(1)} %bitcast.4, f32[2,4]{1,0:T(2,128)} %mix.5), custom_call_target="tpu_custom_call" | custom-call | tf_op jit(solution)/shard_map/pallas_call | solution.py:219

commit v4 on v3

--- a/solution.py
+++ b/solution.py
@@ -24,8 +24,9 @@
     return 1.0 - 2.0 * s * s, 2.0 * s + 2.0 * s * c
 
 
-def angle(mix_ref, layer, group, width=128):
-    return trig(jnp.full((1, width), mix_ref[layer, group], jnp.float32))
+def angle(turns, layer, group):
+    k = layer * 4 + group
+    return turns[k : k + 1, :], turns[8 + k : 9 + k, :]
 
 
 def iota(shape, dim):
@@ -98,12 +99,18 @@
     return bit(p, 0) == 1, 1.0 - 2.0 * bit(p, 1).astype(jnp.float32)
 
 
-def first_kernel(amp, en, ph, mix, out):
+def first_kernel(amp_in, en_in, ph_in, mix_in, out, turns, amp, en, ph, mix, sems):
+    copies = [(mix_in, mix), (ph_in, ph), (en_in, en), (amp_in, amp)]
+    copies = [pltpu.make_async_copy(a, b, sems.at[k]) for k, (a, b) in enumerate(copies)]
+    for copy in copies:
+        copy.start()
     own = own_pop()
-    turns = [quarter_turns(own + k) for k in range(3)]
+    quarters = [quarter_turns(own + k) for k in range(3)]
+    for copy in copies:
+        copy.wait()
     xr, xi = [], []
     for t in range(4):
-        odd, sign = turns[bin(t).count("1")]
+        odd, sign = quarters[bin(t).count("1")]
         e = en[t]
         c, s = trig(ph[0:1, :] * e)
         c, s = jnp.where(odd, -s, c) * sign, jnp.where(odd, c, s) * sign
@@ -113,11 +120,18 @@
         e2 = (ph[1:2, :] * e).T
         for lb in range(2):
             out[pl.ds(t * 64 * 6 + 4 + lb, 64, stride=6), :] = e2[lb * 64 : lb * 64 + 64]
+    row = iota((8, 128), 0)
+    b = jnp.zeros((8, 128), jnp.float32)
+    for k in range(8):
+        b = jnp.where(row == k, mix[k // 4, k % 4], b)
+    c, s = trig(b)
+    turns[0:8, :] = c
+    turns[8:16, :] = s
     bits = range(7)
-    c2, s2 = angle(mix, 0, 2)
-    c, s = angle(mix, 0, 0)
+    c2, s2 = angle(turns, 0, 2)
+    c, s = angle(turns, 0, 0)
     lanes = doubled(table([(k, k, ROT_T, c, s) for k in bits]), ROT_T, c2, s2)
-    c, s = angle(mix, 0, 1)
+    c, s = angle(turns, 0, 1)
     rows = doubled(table([(k, k, ROT_T, c, s) for k in bits]), ROT_T, c2, s2)
     x = [jnp.concatenate([v[t], v[t + 1]], axis=1) for v in (xr, xi) for t in (0, 2)]
     y = mm(jnp.concatenate(x, axis=0), lanes)
@@ -137,31 +151,31 @@
                 out[pl.ds(t * 64 * 6 + c * 2 + lb, 64, stride=6), :] = y[at : at + 64, t // 2 * 128 : t // 2 * 128 + 128]
 
 
-def device_bits(mix, layer, kind):
-    c2, s2 = angle(mix, layer, 2)
-    c3, s3 = angle(mix, layer, 3)
+def device_bits(turns, layer, kind):
+    c2, s2 = angle(turns, layer, 2)
+    c3, s3 = angle(turns, layer, 3)
     small = table([(k, k, kind, c2, s2) for k in range(5)] + [(k, k, kind, c3, s3) for k in (5, 6)])
     return doubled(small, kind, c3, s3)
 
 
-def second_kernel(arrived, mix, out):
+def second_kernel(arrived, turns, out):
     x = jnp.concatenate([arrived[pl.ds(k, 256, stride=6), :] for k in range(4)], axis=1)
-    y = mm(device_bits(mix, 0, ROT), x)
+    y = mm(device_bits(turns, 0, ROT), x)
     z = [None] * 4
     for lb in range(2):
         c, s = trig(arrived[pl.ds(4 + lb, 256, stride=6), :])
         re, im = y[:, lb * 128 : lb * 128 + 128], y[:, 256 + lb * 128 : 384 + lb * 128]
         z[lb] = re * c + im * s
         z[2 + lb] = im * c - re * s
-    c1, s1 = angle(mix, 1, 1)
+    c1, s1 = angle(turns, 1, 1)
     moved = (5, 6, 0, 1, 2, 3, 4)
     rows = table([(k, moved[k], FLIP, c1, s1) for k in range(7)])
-    c0, s0 = angle(mix, 1, 0)
+    c0, s0 = angle(turns, 1, 0)
     z = jnp.concatenate(
         [jnp.concatenate(z[:2], axis=1), jnp.concatenate(z[2:], axis=1)], axis=0
     )
     z = mm(z, doubled(rows, FLIP, c0, s0))
-    v = mm(device_bits(mix, 1, FLIP), jnp.concatenate([z[:256], z[256:]], axis=1))
+    v = mm(device_bits(turns, 1, FLIP), jnp.concatenate([z[:256], z[256:]], axis=1))
     v = [v[:, k * 128 : k * 128 + 128] for k in range(4)]
     for k in range(4):
         out[pl.ds(k, 256, stride=8), :] = v[k]
@@ -171,17 +185,17 @@
             out[pl.ds(m * 256 + 4 + q, 32, stride=8), :] = a[q * 32 : q * 32 + 32]
 
 
-def third_kernel(arrived, mix, final, marginal):
-    c0, s0 = angle(mix, 1, 0)
-    c2, s2 = angle(mix, 1, 2)
+def third_kernel(arrived, turns, final_out, marginal_out, final, marginal, sems):
+    c0, s0 = angle(turns, 1, 0)
+    c2, s2 = angle(turns, 1, 2)
     small = table([(k, k, FLIP, c0, s0) for k in range(6)] + [(6, 6, FLIP, c2, s2)])
     w = doubled(small, FLIP, c2, s2)
-    x = jnp.concatenate([arrived[pl.ds(k, 256, stride=8), :] for k in range(8)], axis=1)
-    y = mm(w, x)
+    y = mm(w, jnp.concatenate([arrived[pl.ds(k, 256, stride=8), :] for k in range(4)], axis=1))
     own = own_pop()
-    turns = [quarter_turns(own + k) for k in range(3)]
+    quarters = [quarter_turns(own + k) for k in range(3)]
+    copies = []
     for t in range(4):
-        odd, sign = turns[bin(t).count("1")]
+        odd, sign = quarters[bin(t).count("1")]
         f = []
         for c in range(2):
             part = [y[t * 64 : t * 64 + 64, (c * 2 + lb) * 128 : (c * 2 + lb) * 128 + 128] for lb in range(2)]
@@ -190,10 +204,13 @@
         for q in range(4):
             final[0, t, pl.ds(q, 32, stride=4), :] = re[q * 32 : q * 32 + 32]
             final[1, t, pl.ds(q, 32, stride=4), :] = im[q * 32 : q * 32 + 32]
+        copies.append(pltpu.make_async_copy(final.at[:, t], final_out.at[:, t], sems.at[t]))
+        copies[t].start()
+    y = mm(w, jnp.concatenate([arrived[pl.ds(4 + k, 256, stride=8), :] for k in range(4)], axis=1))
     pick = jnp.where(bit(iota((8, 128), 1), 5) == iota((8, 128), 0), 1.0 / 32.0, 0.0).astype(jnp.bfloat16)
     upper = iota((1, 128), 1) >= 64
     for q in range(4):
-        chance = y[:, (4 + q) * 128 : (5 + q) * 128]
+        chance = y[:, q * 128 : q * 128 + 128]
         high, low = halves(chance * chance)
         total = lax.dot_general(
             jnp.concatenate([pick, pick], axis=1),
@@ -206,42 +223,58 @@
             moved = pltpu.roll(part, 64, 1)
             first, second = (moved, part) if t % 2 else (part, moved)
             marginal[t, q : q + 1, :] = jnp.where(upper, second[1:2], first[0:1])
-
-
-def full(shape):
-    return pl.BlockSpec(shape, lambda: (0,) * len(shape))
-
-
-def call(body, outs, *args, inner=False):
-    specs = [
-        pl.BlockSpec(memory_space=pltpu.SMEM) if a.shape == (2, 4) else pl.BlockSpec(memory_space=pltpu.VMEM) if a.shape[0] > 1000 else full(a.shape) for a in args
-    ]
-    return pl.pallas_call(
-        body,
-        out_shape=[
-            pltpu.VMEM(s, jnp.float32) if inner else jax.ShapeDtypeStruct(s, jnp.float32) for s in outs
-        ],
-        in_specs=specs,
-        out_specs=[
-            pl.BlockSpec(memory_space=pltpu.VMEM) if inner else full(s) for s in outs
-        ],
-    )(*args)
+    copies.append(pltpu.make_async_copy(marginal, marginal_out, sems.at[4]))
+    copies[4].start()
+    for copy in copies:
+        copy.wait()
+
+
+HERE, AWAY = pl.BlockSpec(memory_space=pltpu.VMEM), pl.BlockSpec(memory_space=pl.ANY)
+
+
+def inner(*shape):
+    return pltpu.VMEM(shape, jnp.float32)
+
+
+def kept(value):
+    return pltpu.with_memory_space_constraint(value, pltpu.VMEM)
 
 
 def exchange(values, *chunk):
     moved = lax.all_to_all(values.reshape(256, *chunk), GROUP, 0, 0, tiled=True)
-    return pltpu.with_memory_space_constraint(moved.reshape(values.shape), pltpu.VMEM)
+    return kept(moved.reshape(values.shape))
 
 
 def on_device(amplitudes, energies, phase_angles, mix_angles):
-    (sent,) = call(first_kernel, [(1536, 128)], amplitudes, energies, phase_angles, mix_angles, inner=True)
+    sent, turns = pl.pallas_call(
+        first_kernel,
+        out_shape=[inner(1536, 128), inner(16, 128)],
+        in_specs=[AWAY] * 4,
+        out_specs=[HERE, HERE],
+        scratch_shapes=[
+            inner(2, 4, 128, 128),
+            inner(4, 128, 128),
+            inner(2, 128),
+            pltpu.SMEM((2, 4), jnp.float32),
+            pltpu.SemaphoreType.DMA((4,)),
+        ],
+    )(amplitudes, energies, phase_angles, mix_angles)
+    turns = kept(turns)
     arrived = exchange(sent, 3, 2, 128)
-    (sent,) = call(second_kernel, [(2048, 128)], arrived, mix_angles, inner=True)
+    sent = pl.pallas_call(
+        second_kernel, out_shape=inner(2048, 128), in_specs=[HERE, HERE], out_specs=HERE
+    )(arrived, turns)
     arrived = exchange(sent, 8, 128)
-    final, marginal = call(
-        third_kernel, [(2, 4, 128, 128), (4, 4, 128)], arrived, mix_angles
-    )
-    return final, marginal
+    return pl.pallas_call(
+        third_kernel,
+        out_shape=[
+            jax.ShapeDtypeStruct((2, 4, 128, 128), jnp.float32),
+            jax.ShapeDtypeStruct((4, 4, 128), jnp.float32),
+        ],
+        in_specs=[HERE, HERE],
+        out_specs=[AWAY, AWAY],
+        scratch_shapes=[inner(2, 4, 128, 128), inner(4, 4, 128), pltpu.SemaphoreType.DMA((5,))],
+    )(arrived, turns)
 
 
 def solution(mesh):

time: 86.8 us -> 85.4 us (0.984)
  Pallas kernels: 7.28 us -> 5.83 us
    pallas_call x3, Pallas kernels: 7.28 us -> 5.83 us  [the longest x1 2.54 us: on_device(): pl.pallas_call(first_kernel, out_shape=[inner(1536, 128), inner(16, 128)]...]
where the time goes in v4:
time: 85.4 us; the launch traced here: 85.2 us
  blocking collectives  78.7 us (92%)
  Pallas kernels  5.83 us (7%)
    all_to_all x2, blocking collectives, exchange(): moved = lax.all_to_all(values.reshape(256, *chunk), GROUP, 0, 0, tiled=True)  78.7 us
    pallas_call x1, Pallas kernels, on_device(): pl.pallas_call(first_kernel, out_shape=[inner(1536, 128), inner(16, 128)]...  2.54 us

profile of v4, /device:TPU:1, one launch (start us, length us, event | category | flops | bytes accessed | tf_op | source)
XLA Modules:
  0.0 85.2 jit_solution(6955739937729285619)
XLA Ops:
  0.6 2.5 %shard_map.59 = (f32[1536,128]{1,0:T(8,128)S(1)}, f32[16,128]{1,0:T(8,128)S(1)}) custom-call(f32[2,4,128,128]{3,2,1,0:T(8,128)} %amp_in.1, f32[4,128,128]{2,1,0:T(8,128)} %en_in.1, f32[2,128]{1,0:T(2,128)} %ph_in.1, f32[2,4]{1,0:T(2,128)} %mix_in.1), custom_call_target="tpu_custom_call" | custom-call | tf_op jit(solution)/shard_map/pallas_call | solution.py:249
  3.2 42.0 %all_to_all.10 = f32[256,3,2,128]{3,2,1,0:T(2,128)S(1)} all-to-all(f32[256,3,2,128]{3,2,1,0:T(2,128)S(1)} %bitcast.7), channel_id=1, replica_groups=mesh['bank'=32,'lane'=8] {'lane','bank'}, dimensions={0} | all-to-all | bytes 1572864 | tf_op jit(solution)/shard_map/all_to_all | solution.py:244
  45.2 1.6 %shard_map.60 = f32[2048,128]{1,0:T(8,128)S(1)} custom-call(f32[1536,128]{1,0:T(8,128)S(1)} %bitcast.6, f32[16,128]{1,0:T(8,128)S(1)} %get-tuple-element.5.turns), custom_call_target="tpu_custom_call" | custom-call | tf_op jit(solution)/shard_map/pallas_call | solution.py:264
  46.8 36.8 %all_to_all.11 = f32[256,8,128]{2,1,0:T(8,128)S(1)} all-to-all(f32[256,8,128]{2,1,0:T(8,128)S(1)} %bitcast.4), channel_id=1, replica_groups=mesh['bank'=32,'lane'=8] {'lane','bank'}, dimensions={0} | all-to-all | bytes 2097152 | tf_op jit(solution)/shard_map/all_to_all | solution.py:244
  83.6 1.6 %shard_map.61 = (f32[2,4,128,128]{3,2,1,0:T(8,128)}, f32[4,4,128]{2,1,0:T(4,128)}) custom-call(f32[2048,128]{1,0:T(8,128)S(1)} %bitcast.5, f32[16,128]{1,0:T(8,128)S(1)} %get-tuple-element.5.turns), custom_call_target="tpu_custom_call" | custom-call | tf_op jit(solution)/shard_map/pallas_call | solution.py:268

commit v5 on v4

--- a/solution.py
+++ b/solution.py
@@ -3,11 +3,12 @@
 from jax import lax
 from jax.experimental import pallas as pl
 from jax.experimental.pallas import tpu as pltpu
-from jax.sharding import PartitionSpec as P
+from jax.sharding import Mesh, PartitionSpec as P
 
 
 ROT, ROT_T, FLIP = 0, 1, 2
-GROUP = ("lane", "bank")
+AXES = ("zh", "y", "x", "zl", "core")
+GROUP = ("zh", "zl", "y", "x", "core")
 
 
 def trig(x):
@@ -52,11 +53,13 @@
     return c, s, s, -c
 
 
-def table(pairs):
-    j = iota((1, 128), 1)
+def table(pairs, width=128):
+    j = iota((1, width), 1)
     i = iota((8, 1), 0)
-    out = jnp.ones((8, 128), jnp.float32)
+    out = jnp.ones((8, width), jnp.float32)
     for k, kj, kind, c, s in pairs:
+        if width > 128:
+            c, s = jnp.concatenate([c, c], axis=1), jnp.concatenate([s, s], axis=1)
         a00, a01, a10, a11 = pair(kind, c, s)
         odd = bit(j, kj) == 1
         upper, lower = jnp.where(odd, a01, a00), jnp.where(odd, a11, a10)
@@ -90,7 +93,7 @@
 
 
 def own_pop():
-    return pop(lax.axis_index("bank"), 5) + pop(lax.axis_index("lane"), 3)
+    return sum(pop(lax.axis_index(axis), 1 if axis in ("zh", "core") else 2) for axis in AXES)
 
 
 def quarter_turns(extra):
@@ -151,16 +154,17 @@
                 out[pl.ds(t * 64 * 6 + c * 2 + lb, 64, stride=6), :] = y[at : at + 64, t // 2 * 128 : t // 2 * 128 + 128]
 
 
-def device_bits(turns, layer, kind):
-    c2, s2 = angle(turns, layer, 2)
-    c3, s3 = angle(turns, layer, 3)
-    small = table([(k, k, kind, c2, s2) for k in range(5)] + [(k, k, kind, c3, s3) for k in (5, 6)])
-    return doubled(small, kind, c3, s3)
+MIDDLE = (0, 5, 6)
+SORTED = (1, 2, 3, 4, 7, 0, 5, 6)
+
+
+def device_bits(turns, layer, kind, order):
+    return table([(k, kj, kind, *angle(turns, layer, 3 if kj in MIDDLE else 2)) for k, kj in enumerate(order)], 256)
 
 
 def second_kernel(arrived, turns, out):
     x = jnp.concatenate([arrived[pl.ds(k, 256, stride=6), :] for k in range(4)], axis=1)
-    y = mm(device_bits(turns, 0, ROT), x)
+    y = mm(device_bits(turns, 0, ROT, range(8)), x)
     z = [None] * 4
     for lb in range(2):
         c, s = trig(arrived[pl.ds(4 + lb, 256, stride=6), :])
@@ -175,14 +179,19 @@
         [jnp.concatenate(z[:2], axis=1), jnp.concatenate(z[2:], axis=1)], axis=0
     )
     z = mm(z, doubled(rows, FLIP, c0, s0))
-    v = mm(device_bits(turns, 1, FLIP), jnp.concatenate([z[:256], z[256:]], axis=1))
+    v = mm(device_bits(turns, 1, FLIP, SORTED), jnp.concatenate([z[:256], z[256:]], axis=1))
     v = [v[:, k * 128 : k * 128 + 128] for k in range(4)]
-    for k in range(4):
-        out[pl.ds(k, 256, stride=8), :] = v[k]
     for m in range(8):
+        to = [(zh * 128 + (m // 2) * 32 + m % 2) * 8 for zh in range(2)]
+        for k in range(4):
+            for zh in range(2):
+                at = m * 32 + zh * 16
+                out[pl.ds(to[zh] + k, 16, stride=16), :] = v[k][at : at + 16]
         a = jnp.concatenate([v[k][m * 32 : m * 32 + 32] for k in range(4)], axis=0).T
         for q in range(4):
-            out[pl.ds(m * 256 + 4 + q, 32, stride=8), :] = a[q * 32 : q * 32 + 32]
+            for zh in range(2):
+                at = q * 32 + zh * 16
+                out[pl.ds(to[zh] + 4 + q, 16, stride=16), :] = a[at : at + 16]
 
 
 def third_kernel(arrived, turns, final_out, marginal_out, final, marginal, sems):
@@ -278,11 +287,11 @@
 
 
 def solution(mesh):
-    placed = (P(None, ("bank", "lane"), None, None), P(("bank", "lane"), None, None), P(), P())
+    parted = Mesh(mesh.devices.reshape(2, 4, 4, 4, 2), AXES)
     return jax.shard_map(
         on_device,
-        mesh=mesh,
-        in_specs=placed,
-        out_specs=(P(None, ("bank", "lane"), None, None), P("lane", "bank", None)),
+        mesh=parted,
+        in_specs=(P(None, AXES, None, None), P(AXES, None, None), P(), P()),
+        out_specs=(P(None, AXES, None, None), P(AXES[3:], AXES[:3], None)),
         check_vma=False,
     )

time: 85.4 us -> 84 us (0.984)
  blocking collectives: 78.7 us -> 77.3 us
    all_to_all x2, blocking collectives: 78.7 us -> 77.3 us  [exchange(): moved = lax.all_to_all(values.reshape(256, *chunk), GROUP, 0, 0, tiled=True)]
where the time goes in v5:
time: 84 us; the launch traced here: 83.8 us
  blocking collectives  77.3 us (92%)
  Pallas kernels  5.91 us (7%)
    all_to_all x2, blocking collectives, exchange(): moved = lax.all_to_all(values.reshape(256, *chunk), GROUP, 0, 0, tiled=True)  77.3 us
    pallas_call x1, Pallas kernels, on_device(): pl.pallas_call(first_kernel, out_shape=[inner(1536, 128), inner(16, 128)]...  2.54 us
    pallas_call x1, Pallas kernels, on_device(): pl.pallas_call(second_kernel, out_shape=inner(2048, 128), in_specs=[HERE,...  1.71 us

profile of v5, /device:TPU:1, one launch (start us, length us, event | category | flops | bytes accessed | tf_op | source)
XLA Modules:
  0.0 83.8 jit_solution(16311117793406468769)
XLA Ops:
  0.6 2.5 %shard_map.59 = (f32[1536,128]{1,0:T(8,128)S(1)}, f32[16,128]{1,0:T(8,128)S(1)}) custom-call(f32[2,4,128,128]{3,2,1,0:T(8,128)} %amp_in.1, f32[4,128,128]{2,1,0:T(8,128)} %en_in.1, f32[2,128]{1,0:T(2,128)} %ph_in.1, f32[2,4]{1,0:T(2,128)} %mix_in.1), custom_call_target="tpu_custom_call" | custom-call | tf_op jit(solution)/shard_map/pallas_call | solution.py:258
  3.2 40.8 %all_to_all.10 = f32[256,3,2,128]{3,2,1,0:T(2,128)S(1)} all-to-all(f32[256,3,2,128]{3,2,1,0:T(2,128)S(1)} %bitcast.7), channel_id=1, replica_groups=mesh['zh'=2,'y'=4,'x'=4,'zl'=4,'core'=2] {'zh','zl','y','x','core'}, dimensions={0} | all-to-all | bytes 1572864 | tf_op jit(solution)/shard_map/all_to_all | solution.py:253
  44.0 1.7 %shard_map.60 = f32[2048,128]{1,0:T(8,128)S(1)} custom-call(f32[1536,128]{1,0:T(8,128)S(1)} %bitcast.6, f32[16,128]{1,0:T(8,128)S(1)} %get-tuple-element.5.turns), custom_call_target="tpu_custom_call" | custom-call | tf_op jit(solution)/shard_map/pallas_call | solution.py:273
  45.7 36.5 %all_to_all.11 = f32[256,8,128]{2,1,0:T(8,128)S(1)} all-to-all(f32[256,8,128]{2,1,0:T(8,128)S(1)} %bitcast.4), channel_id=1, replica_groups=mesh['zh'=2,'y'=4,'x'=4,'zl'=4,'core'=2] {'zh','zl','y','x','core'}, dimensions={0} | all-to-all | bytes 2097152 | tf_op jit(solution)/shard_map/all_to_all | solution.py:253
  82.2 1.6 %shard_map.61 = (f32[2,4,128,128]{3,2,1,0:T(8,128)}, f32[4,4,128]{2,1,0:T(4,128)}) custom-call(f32[2048,128]{1,0:T(8,128)S(1)} %bitcast.5, f32[16,128]{1,0:T(8,128)S(1)} %get-tuple-element.5.turns), custom_call_target="tpu_custom_call" | custom-call | tf_op jit(solution)/shard_map/pallas_call | solution.py:277

commit v6 on v5

--- a/solution.py
+++ b/solution.py
@@ -11,18 +11,17 @@
 GROUP = ("zh", "zl", "y", "x", "core")
 
 
-def trig(x):
-    h = x * 0.5
+def trig(h):
     y = h * h
-    c = jnp.full_like(x, 1.0 / 479001600.0)
-    s = jnp.full_like(x, 1.0 / 6227020800.0)
-    for k in (-3628800.0, 40320.0, -720.0, 24.0, -2.0):
+    c = jnp.full_like(h, -1.0 / 3628800.0)
+    s = jnp.full_like(h, -1.0 / 39916800.0)
+    for k in (40320.0, -720.0, 24.0, -2.0):
         c = c * y + 1.0 / k
-    for k in (-39916800.0, 362880.0, -5040.0, 120.0, -6.0, 1.0):
+    for k in (362880.0, -5040.0, 120.0, -6.0, 1.0):
         s = s * y + 1.0 / k
     s = s * h
-    c = c * y
-    return 1.0 - 2.0 * s * s, 2.0 * s + 2.0 * s * c
+    twice = s + s
+    return 1.0 - twice * s, twice + twice * (c * y)
 
 
 def angle(turns, layer, group):
@@ -83,13 +82,13 @@
 
 
 def mm(a, b):
-    ah, al = halves(a)
     bh, bl = halves(b)
-    return jnp.dot(
-        jnp.concatenate([ah, ah, al], axis=1),
-        jnp.concatenate([bh, bl, bh], axis=0),
-        preferred_element_type=jnp.float32,
-    )
+    b = jnp.concatenate([bh, bl, bh], axis=0)
+    out = []
+    for part in jnp.split(a, 2, axis=0):
+        ah, al = halves(part)
+        out.append(jnp.dot(jnp.concatenate([ah, ah, al], axis=1), b, preferred_element_type=jnp.float32))
+    return jnp.concatenate(out, axis=0)
 
 
 def own_pop():
@@ -97,9 +96,10 @@
 
 
 def quarter_turns(extra):
-    shape = (128, 128)
-    p = pop(iota(shape, 0), 7) + pop(iota(shape, 1), 7) + extra
-    return bit(p, 0) == 1, 1.0 - 2.0 * bit(p, 1).astype(jnp.float32)
+    p = pop(iota((8, 128), 0), 3) + pop(iota((8, 128), 1), 7) + extra
+    kinds = [(bit(p + k, 0), 1.0 - 2.0 * bit(p + k, 1).astype(jnp.float32)) for k in range(4)]
+    kinds = [kinds[bin(v).count("1") % 4] for v in range(16)]
+    return [jnp.concatenate(part, axis=0) for part in zip(*kinds)]
 
 
 def first_kernel(amp_in, en_in, ph_in, mix_in, out, turns, amp, en, ph, mix, sems):
@@ -111,23 +111,25 @@
     quarters = [quarter_turns(own + k) for k in range(3)]
     for copy in copies:
         copy.wait()
+    half = ph[...] * 0.5
     xr, xi = [], []
     for t in range(4):
         odd, sign = quarters[bin(t).count("1")]
+        odd = odd == 1
         e = en[t]
-        c, s = trig(ph[0:1, :] * e)
+        c, s = trig(half[0:1] * e)
         c, s = jnp.where(odd, -s, c) * sign, jnp.where(odd, c, s) * sign
         re, im = amp[0, t], amp[1, t]
         xr.append(re * c + im * s)
         xi.append(im * c - re * s)
-        e2 = (ph[1:2, :] * e).T
+        e2 = (half[1:2] * e).T
         for lb in range(2):
             out[pl.ds(t * 64 * 6 + 4 + lb, 64, stride=6), :] = e2[lb * 64 : lb * 64 + 64]
     row = iota((8, 128), 0)
     b = jnp.zeros((8, 128), jnp.float32)
     for k in range(8):
         b = jnp.where(row == k, mix[k // 4, k % 4], b)
-    c, s = trig(b)
+    c, s = trig(b * 0.5)
     turns[0:8, :] = c
     turns[8:16, :] = s
     bits = range(7)
@@ -205,6 +207,7 @@
     copies = []
     for t in range(4):
         odd, sign = quarters[bin(t).count("1")]
+        odd = odd == 1
         f = []
         for c in range(2):
             part = [y[t * 64 : t * 64 + 64, (c * 2 + lb) * 128 : (c * 2 + lb) * 128 + 128] for lb in range(2)]

time: 84 us -> 83.3 us (level)
  no operation moved by 1% of the time
where the time goes in v6:
time: 83.3 us; the launch traced here: 83.2 us
  blocking collectives  77.3 us (93%)
  Pallas kernels  5.23 us (6%)
    all_to_all x2, blocking collectives, exchange(): moved = lax.all_to_all(values.reshape(256, *chunk), GROUP, 0, 0, tiled=True)  77.3 us
    pallas_call x1, Pallas kernels, on_device(): pl.pallas_call(first_kernel, out_shape=[inner(1536, 128), inner(16, 128)]...  2.28 us

profile of v6, /device:TPU:1, one launch (start us, length us, event | category | flops | bytes accessed | tf_op | source)
XLA Modules:
  0.0 83.2 jit_solution(18051402466969374369)
XLA Ops:
  0.6 2.3 %shard_map.59 = (f32[1536,128]{1,0:T(8,128)S(1)}, f32[16,128]{1,0:T(8,128)S(1)}) custom-call(f32[2,4,128,128]{3,2,1,0:T(8,128)} %amp_in.1, f32[4,128,128]{2,1,0:T(8,128)} %en_in.1, f32[2,128]{1,0:T(2,128)} %ph_in.1, f32[2,4]{1,0:T(2,128)} %mix_in.1), custom_call_target="tpu_custom_call" | custom-call | tf_op jit(solution)/shard_map/pallas_call | solution.py:261
  2.9 40.8 %all_to_all.10 = f32[256,3,2,128]{3,2,1,0:T(2,128)S(1)} all-to-all(f32[256,3,2,128]{3,2,1,0:T(2,128)S(1)} %bitcast.7), channel_id=1, replica_groups=mesh['zh'=2,'y'=4,'x'=4,'zl'=4,'core'=2] {'zh','zl','y','x','core'}, dimensions={0} | all-to-all | bytes 1572864 | tf_op jit(solution)/shard_map/all_to_all | solution.py:256
  43.7 1.4 %shard_map.60 = f32[2048,128]{1,0:T(8,128)S(1)} custom-call(f32[1536,128]{1,0:T(8,128)S(1)} %bitcast.6, f32[16,128]{1,0:T(8,128)S(1)} %get-tuple-element.5.turns), custom_call_target="tpu_custom_call" | custom-call | tf_op jit(solution)/shard_map/pallas_call | solution.py:276
  45.1 36.5 %all_to_all.11 = f32[256,8,128]{2,1,0:T(8,128)S(1)} all-to-all(f32[256,8,128]{2,1,0:T(8,128)S(1)} %bitcast.4), channel_id=1, replica_groups=mesh['zh'=2,'y'=4,'x'=4,'zl'=4,'core'=2] {'zh','zl','y','x','core'}, dimensions={0} | all-to-all | bytes 2097152 | tf_op jit(solution)/shard_map/all_to_all | solution.py:256
  81.6 1.6 %shard_map.61 = (f32[2,4,128,128]{3,2,1,0:T(8,128)}, f32[4,4,128]{2,1,0:T(4,128)}) custom-call(f32[2048,128]{1,0:T(8,128)S(1)} %bitcast.5, f32[16,128]{1,0:T(8,128)S(1)} %get-tuple-element.5.turns), custom_call_target="tpu_custom_call" | custom-call | tf_op jit(solution)/shard_map/pallas_call | solution.py:280

commit v7 on v6

--- a/solution.py
+++ b/solution.py
@@ -109,7 +109,21 @@
         copy.start()
     own = own_pop()
     quarters = [quarter_turns(own + k) for k in range(3)]
-    for copy in copies:
+    copies[0].wait()
+    row = iota((8, 128), 0)
+    b = jnp.zeros((8, 128), jnp.float32)
+    for k in range(8):
+        b = jnp.where(row == k, mix[k // 4, k % 4], b)
+    c, s = trig(b * 0.5)
+    turns[0:8, :] = c
+    turns[8:16, :] = s
+    bits = range(7)
+    c2, s2 = angle(turns, 0, 2)
+    c, s = angle(turns, 0, 0)
+    lanes = doubled(table([(k, k, ROT_T, c, s) for k in bits]), ROT_T, c2, s2)
+    c, s = angle(turns, 0, 1)
+    rows = doubled(table([(k, k, ROT_T, c, s) for k in bits]), ROT_T, c2, s2)
+    for copy in copies[1:]:
         copy.wait()
     half = ph[...] * 0.5
     xr, xi = [], []
@@ -125,19 +139,6 @@
         e2 = (half[1:2] * e).T
         for lb in range(2):
             out[pl.ds(t * 64 * 6 + 4 + lb, 64, stride=6), :] = e2[lb * 64 : lb * 64 + 64]
-    row = iota((8, 128), 0)
-    b = jnp.zeros((8, 128), jnp.float32)
-    for k in range(8):
-        b = jnp.where(row == k, mix[k // 4, k % 4], b)
-    c, s = trig(b * 0.5)
-    turns[0:8, :] = c
-    turns[8:16, :] = s
-    bits = range(7)
-    c2, s2 = angle(turns, 0, 2)
-    c, s = angle(turns, 0, 0)
-    lanes = doubled(table([(k, k, ROT_T, c, s) for k in bits]), ROT_T, c2, s2)
-    c, s = angle(turns, 0, 1)
-    rows = doubled(table([(k, k, ROT_T, c, s) for k in bits]), ROT_T, c2, s2)
     x = [jnp.concatenate([v[t], v[t + 1]], axis=1) for v in (xr, xi) for t in (0, 2)]
     y = mm(jnp.concatenate(x, axis=0), lanes)
     z = []

time: 83.3 us -> 83.3 us (level)
  no operation moved by 1% of the time
where the time goes in v7:
time: 83.3 us; the launch traced here: 83.1 us
  blocking collectives  77.3 us (93%)
  Pallas kernels  5.19 us (6%)
    all_to_all x2, blocking collectives, exchange(): moved = lax.all_to_all(values.reshape(256, *chunk), GROUP, 0, 0, tiled=True)  77.3 us
    pallas_call x1, Pallas kernels, on_device(): pl.pallas_call(first_kernel, out_shape=[inner(1536, 128), inner(16, 128)]...  2.24 us

profile of v7, /device:TPU:1, one launch (start us, length us, event | category | flops | bytes accessed | tf_op | source)
XLA Modules:
  0.0 83.1 jit_solution(16112000394646678299)
XLA Ops:
  0.6 2.2 %shard_map.59 = (f32[1536,128]{1,0:T(8,128)S(1)}, f32[16,128]{1,0:T(8,128)S(1)}) custom-call(f32[2,4,128,128]{3,2,1,0:T(8,128)} %amp_in.1, f32[4,128,128]{2,1,0:T(8,128)} %en_in.1, f32[2,128]{1,0:T(2,128)} %ph_in.1, f32[2,4]{1,0:T(2,128)} %mix_in.1), custom_call_target="tpu_custom_call" | custom-call | tf_op jit(solution)/shard_map/pallas_call | solution.py:262
  2.9 40.8 %all_to_all.10 = f32[256,3,2,128]{3,2,1,0:T(2,128)S(1)} all-to-all(f32[256,3,2,128]{3,2,1,0:T(2,128)S(1)} %bitcast.7), channel_id=1, replica_groups=mesh['zh'=2,'y'=4,'x'=4,'zl'=4,'core'=2] {'zh','zl','y','x','core'}, dimensions={0} | all-to-all | bytes 1572864 | tf_op jit(solution)/shard_map/all_to_all | solution.py:257
  43.7 1.4 %shard_map.60 = f32[2048,128]{1,0:T(8,128)S(1)} custom-call(f32[1536,128]{1,0:T(8,128)S(1)} %bitcast.6, f32[16,128]{1,0:T(8,128)S(1)} %get-tuple-element.5.turns), custom_call_target="tpu_custom_call" | custom-call | tf_op jit(solution)/shard_map/pallas_call | solution.py:277
  45.0 36.5 %all_to_all.11 = f32[256,8,128]{2,1,0:T(8,128)S(1)} all-to-all(f32[256,8,128]{2,1,0:T(8,128)S(1)} %bitcast.4), channel_id=1, replica_groups=mesh['zh'=2,'y'=4,'x'=4,'zl'=4,'core'=2] {'zh','zl','y','x','core'}, dimensions={0} | all-to-all | bytes 2097152 | tf_op jit(solution)/shard_map/all_to_all | solution.py:257
  81.5 1.6 %shard_map.61 = (f32[2,4,128,128]{3,2,1,0:T(8,128)}, f32[4,4,128]{2,1,0:T(4,128)}) custom-call(f32[2048,128]{1,0:T(8,128)S(1)} %bitcast.5, f32[16,128]{1,0:T(8,128)S(1)} %get-tuple-element.5.turns), custom_call_target="tpu_custom_call" | custom-call | tf_op jit(solution)/shard_map/pallas_call | solution.py:281

commit v8 on v7

--- a/solution.py
+++ b/solution.py
@@ -85,7 +85,7 @@
     bh, bl = halves(b)
     b = jnp.concatenate([bh, bl, bh], axis=0)
     out = []
-    for part in jnp.split(a, 2, axis=0):
+    for part in jnp.split(a, 4 if a.shape[0] > 256 else 2, axis=0):
         ah, al = halves(part)
         out.append(jnp.dot(jnp.concatenate([ah, ah, al], axis=1), b, preferred_element_type=jnp.float32))
     return jnp.concatenate(out, axis=0)

time: 83.3 us -> 83.1 us (level)
  no operation moved by 1% of the time
where the time goes in v8:
time: 83.1 us; the launch traced here: 83 us
  blocking collectives  77.3 us (93%)
  Pallas kernels  5.04 us (6%)
    all_to_all x2, blocking collectives, exchange(): moved = lax.all_to_all(values.reshape(256, *chunk), GROUP, 0, 0, tiled=True)  77.3 us
    pallas_call x1, Pallas kernels, on_device(): pl.pallas_call(first_kernel, out_shape=[inner(1536, 128), inner(16, 128)]...  2.14 us

profile of v8, /device:TPU:1, one launch (start us, length us, event | category | flops | bytes accessed | tf_op | source)
XLA Modules:
  0.0 83.0 jit_solution(14549841631376681649)
XLA Ops:
  0.6 2.1 %shard_map.59 = (f32[1536,128]{1,0:T(8,128)S(1)}, f32[16,128]{1,0:T(8,128)S(1)}) custom-call(f32[2,4,128,128]{3,2,1,0:T(8,128)} %amp_in.1, f32[4,128,128]{2,1,0:T(8,128)} %en_in.1, f32[2,128]{1,0:T(2,128)} %ph_in.1, f32[2,4]{1,0:T(2,128)} %mix_in.1), custom_call_target="tpu_custom_call" | custom-call | tf_op jit(solution)/shard_map/pallas_call | solution.py:262
  2.8 40.8 %all_to_all.10 = f32[256,3,2,128]{3,2,1,0:T(2,128)S(1)} all-to-all(f32[256,3,2,128]{3,2,1,0:T(2,128)S(1)} %bitcast.7), channel_id=1, replica_groups=mesh['zh'=2,'y'=4,'x'=4,'zl'=4,'core'=2] {'zh','zl','y','x','core'}, dimensions={0} | all-to-all | bytes 1572864 | tf_op jit(solution)/shard_map/all_to_all | solution.py:257
  43.6 1.3 %shard_map.60 = f32[2048,128]{1,0:T(8,128)S(1)} custom-call(f32[1536,128]{1,0:T(8,128)S(1)} %bitcast.6, f32[16,128]{1,0:T(8,128)S(1)} %get-tuple-element.5.turns), custom_call_target="tpu_custom_call" | custom-call | tf_op jit(solution)/shard_map/pallas_call | solution.py:277
  44.9 36.5 %all_to_all.11 = f32[256,8,128]{2,1,0:T(8,128)S(1)} all-to-all(f32[256,8,128]{2,1,0:T(8,128)S(1)} %bitcast.4), channel_id=1, replica_groups=mesh['zh'=2,'y'=4,'x'=4,'zl'=4,'core'=2] {'zh','zl','y','x','core'}, dimensions={0} | all-to-all | bytes 2097152 | tf_op jit(solution)/shard_map/all_to_all | solution.py:257
  81.4 1.6 %shard_map.61 = (f32[2,4,128,128]{3,2,1,0:T(8,128)}, f32[4,4,128]{2,1,0:T(4,128)}) custom-call(f32[2048,128]{1,0:T(8,128)S(1)} %bitcast.5, f32[16,128]{1,0:T(8,128)S(1)} %get-tuple-element.5.turns), custom_call_target="tpu_custom_call" | custom-call | tf_op jit(solution)/shard_map/pallas_call | solution.py:281

commit v9 on v8

--- a/solution.py
+++ b/solution.py
@@ -132,7 +132,8 @@
         odd = odd == 1
         e = en[t]
         c, s = trig(half[0:1] * e)
-        c, s = jnp.where(odd, -s, c) * sign, jnp.where(odd, c, s) * sign
+        flip = jnp.where(odd, -sign, sign)
+        c, s = jnp.where(odd, s, c) * flip, jnp.where(odd, c, s) * sign
         re, im = amp[0, t], amp[1, t]
         xr.append(re * c + im * s)
         xi.append(im * c - re * s)
@@ -213,7 +214,8 @@
         for c in range(2):
             part = [y[t * 64 : t * 64 + 64, (c * 2 + lb) * 128 : (c * 2 + lb) * 128 + 128] for lb in range(2)]
             f.append(jnp.concatenate(part, axis=0).T)
-        re, im = jnp.where(odd, f[1], f[0]) * sign, jnp.where(odd, -f[0], f[1]) * sign
+        flip = jnp.where(odd, -sign, sign)
+        re, im = jnp.where(odd, f[1], f[0]) * sign, jnp.where(odd, f[0], f[1]) * flip
         for q in range(4):
             final[0, t, pl.ds(q, 32, stride=4), :] = re[q * 32 : q * 32 + 32]
             final[1, t, pl.ds(q, 32, stride=4), :] = im[q * 32 : q * 32 + 32]

time: 83.1 us -> 83.1 us (level)
  no operation moved by 1% of the time
where the time goes in v9:
time: 83.1 us; the launch traced here: 83 us
  blocking collectives  77.3 us (93%)
  Pallas kernels  5.04 us (6%)
    all_to_all x2, blocking collectives, exchange(): moved = lax.all_to_all(values.reshape(256, *chunk), GROUP, 0, 0, tiled=True)  77.3 us
    pallas_call x1, Pallas kernels, on_device(): pl.pallas_call(first_kernel, out_shape=[inner(1536, 128), inner(16, 128)]...  2.14 us

profile of v9, /device:TPU:1, one launch (start us, length us, event | category | flops | bytes accessed | tf_op | source)
XLA Modules:
  0.0 83.0 jit_solution(7175626426291166152)
XLA Ops:
  0.6 2.1 %shard_map.59 = (f32[1536,128]{1,0:T(8,128)S(1)}, f32[16,128]{1,0:T(8,128)S(1)}) custom-call(f32[2,4,128,128]{3,2,1,0:T(8,128)} %amp_in.1, f32[4,128,128]{2,1,0:T(8,128)} %en_in.1, f32[2,128]{1,0:T(2,128)} %ph_in.1, f32[2,4]{1,0:T(2,128)} %mix_in.1), custom_call_target="tpu_custom_call" | custom-call | tf_op jit(solution)/shard_map/pallas_call | solution.py:264
  2.8 40.8 %all_to_all.10 = f32[256,3,2,128]{3,2,1,0:T(2,128)S(1)} all-to-all(f32[256,3,2,128]{3,2,1,0:T(2,128)S(1)} %bitcast.7), channel_id=1, replica_groups=mesh['zh'=2,'y'=4,'x'=4,'zl'=4,'core'=2] {'zh','zl','y','x','core'}, dimensions={0} | all-to-all | bytes 1572864 | tf_op jit(solution)/shard_map/all_to_all | solution.py:259
  43.6 1.3 %shard_map.60 = f32[2048,128]{1,0:T(8,128)S(1)} custom-call(f32[1536,128]{1,0:T(8,128)S(1)} %bitcast.6, f32[16,128]{1,0:T(8,128)S(1)} %get-tuple-element.5.turns), custom_call_target="tpu_custom_call" | custom-call | tf_op jit(solution)/shard_map/pallas_call | solution.py:279
  44.9 36.5 %all_to_all.11 = f32[256,8,128]{2,1,0:T(8,128)S(1)} all-to-all(f32[256,8,128]{2,1,0:T(8,128)S(1)} %bitcast.4), channel_id=1, replica_groups=mesh['zh'=2,'y'=4,'x'=4,'zl'=4,'core'=2] {'zh','zl','y','x','core'}, dimensions={0} | all-to-all | bytes 2097152 | tf_op jit(solution)/shard_map/all_to_all | solution.py:259
  81.4 1.6 %shard_map.61 = (f32[2,4,128,128]{3,2,1,0:T(8,128)}, f32[4,4,128]{2,1,0:T(4,128)}) custom-call(f32[2048,128]{1,0:T(8,128)S(1)} %bitcast.5, f32[16,128]{1,0:T(8,128)S(1)} %get-tuple-element.5.turns), custom_call_target="tpu_custom_call" | custom-call | tf_op jit(solution)/shard_map/pallas_call | solution.py:283

commit v10 on v8

--- a/solution.py
+++ b/solution.py
@@ -103,7 +103,7 @@
 
 
 def first_kernel(amp_in, en_in, ph_in, mix_in, out, turns, amp, en, ph, mix, sems):
-    copies = [(mix_in, mix), (ph_in, ph), (en_in, en), (amp_in, amp)]
+    copies = [(mix_in, mix), (ph_in, ph), (en_in, en), (amp_in.at[0], amp.at[0]), (amp_in.at[1], amp.at[1])]
     copies = [pltpu.make_async_copy(a, b, sems.at[k]) for k, (a, b) in enumerate(copies)]
     for copy in copies:
         copy.start()
@@ -269,7 +269,7 @@
             inner(4, 128, 128),
             inner(2, 128),
             pltpu.SMEM((2, 4), jnp.float32),
-            pltpu.SemaphoreType.DMA((4,)),
+            pltpu.SemaphoreType.DMA((5,)),
         ],
     )(amplitudes, energies, phase_angles, mix_angles)
     turns = kept(turns)

time: 83.1 us -> 83.1 us (level)
  no operation moved by 1% of the time
where the time goes in v10:
time: 83.1 us; the launch traced here: 83 us
  blocking collectives  77.3 us (93%)
  Pallas kernels  5.05 us (6%)
    all_to_all x2, blocking collectives, exchange(): moved = lax.all_to_all(values.reshape(256, *chunk), GROUP, 0, 0, tiled=True)  77.3 us
    pallas_call x1, Pallas kernels, on_device(): pl.pallas_call(first_kernel, out_shape=[inner(1536, 128), inner(16, 128)]...  2.14 us

profile of v10, /device:TPU:1, one launch (start us, length us, event | category | flops | bytes accessed | tf_op | source)
XLA Modules:
  0.0 83.0 jit_solution(10810658460942075291)
XLA Ops:
  0.6 2.1 %shard_map.59 = (f32[1536,128]{1,0:T(8,128)S(1)}, f32[16,128]{1,0:T(8,128)S(1)}) custom-call(f32[2,4,128,128]{3,2,1,0:T(8,128)} %amp_in.1, f32[4,128,128]{2,1,0:T(8,128)} %en_in.1, f32[2,128]{1,0:T(2,128)} %ph_in.1, f32[2,4]{1,0:T(2,128)} %mix_in.1), custom_call_target="tpu_custom_call" | custom-call | tf_op jit(solution)/shard_map/pallas_call | solution.py:262
  2.8 40.8 %all_to_all.10 = f32[256,3,2,128]{3,2,1,0:T(2,128)S(1)} all-to-all(f32[256,3,2,128]{3,2,1,0:T(2,128)S(1)} %bitcast.7), channel_id=1, replica_groups=mesh['zh'=2,'y'=4,'x'=4,'zl'=4,'core'=2] {'zh','zl','y','x','core'}, dimensions={0} | all-to-all | bytes 1572864 | tf_op jit(solution)/shard_map/all_to_all | solution.py:257
  43.6 1.3 %shard_map.60 = f32[2048,128]{1,0:T(8,128)S(1)} custom-call(f32[1536,128]{1,0:T(8,128)S(1)} %bitcast.6, f32[16,128]{1,0:T(8,128)S(1)} %get-tuple-element.5.turns), custom_call_target="tpu_custom_call" | custom-call | tf_op jit(solution)/shard_map/pallas_call | solution.py:277
  44.9 36.5 %all_to_all.11 = f32[256,8,128]{2,1,0:T(8,128)S(1)} all-to-all(f32[256,8,128]{2,1,0:T(8,128)S(1)} %bitcast.4), channel_id=1, replica_groups=mesh['zh'=2,'y'=4,'x'=4,'zl'=4,'core'=2] {'zh','zl','y','x','core'}, dimensions={0} | all-to-all | bytes 2097152 | tf_op jit(solution)/shard_map/all_to_all | solution.py:257
  81.4 1.6 %shard_map.61 = (f32[2,4,128,128]{3,2,1,0:T(8,128)}, f32[4,4,128]{2,1,0:T(4,128)}) custom-call(f32[2048,128]{1,0:T(8,128)S(1)} %bitcast.5, f32[16,128]{1,0:T(8,128)S(1)} %get-tuple-element.5.turns), custom_call_target="tpu_custom_call" | custom-call | tf_op jit(solution)/shard_map/pallas_call | solution.py:281
